TPU v7x, 512 devices: a whole 4x8x8 slice. The times are simulated.
512 devices in a mesh: grp: 8 (over z_lo, x), tile: 64 (over z_hi, y, core).
Axes of the slice: x: 4, y: 8, z: 8 (z_hi: 4, z_lo: 2; z = z_hi * 2 + z_lo), core: 2. Of those that a mesh axis runs over, the one named last changes fastest.
Arguments:
- quantized: bfloat16 [16, 384, 8192], P(None, 'grp', 'tile'), may hold values from -6 to 6
- scales: float32 [64, 16, 384], P('tile', None, 'grp'), may hold values from 0.25 to 4
Outputs:
- coefficients: bfloat16 [16, 384, 8192], P(None, 'grp', 'tile')
All inputs are finite; a program needn't handle non-finite values.
Results may differ from a plain program's by a relative error of at most 0.001.
Values sent between devices are 32-bit elements; how exact they have to be, the bound alone decides.
A program may use at most 64 MiB of HBM per device.

v0:
```python
import jax
import jax.numpy as jnp
from jax import lax
from jax.sharding import PartitionSpec as P

QB = 128
LEVELS = 4


LIFT_ALPHA = -1.586134342059924
LIFT_BETA = -0.052980118572961
LIFT_GAMMA = 0.882911075530934
LIFT_DELTA = 0.443506852043971
LIFT_KAPPA = 1.230174104914001
HIGHEST = lax.Precision.HIGHEST


def padded(x, sides, width):
    for axis, dim in sides:
        size, length = (lax.axis_size(axis), x.shape[dim])
        up = [(i, (i + 1) % size) for i in range(size - 1)]
        down = [(j, i) for i, j in up]
        last = lax.slice_in_dim(x, length - width, length, axis=dim)
        initial = lax.slice_in_dim(x, 0, width, axis=dim)
        before = lax.ppermute(last, axis, up)
        after = lax.ppermute(initial, axis, down)
        x = jnp.concatenate([before, x, after], axis=dim)
    return x


def forward_of(values, along):
    length = values.shape[along]
    return jnp.concatenate(
        [
            lax.slice_in_dim(values, 1, length, 1, along),
            lax.slice_in_dim(values, length - 1, length, 1, along),
        ],
        along,
    )


def backward_of(values, along):
    length = values.shape[along]
    return jnp.concatenate(
        [
            lax.slice_in_dim(values, 0, 1, 1, along),
            lax.slice_in_dim(values, 0, length - 1, 1, along),
        ],
        along,
    )


def lift_local(subband, along):
    length = subband.shape[along]
    even_part = lax.slice_in_dim(subband, 0, length, 2, along)
    odd_part = lax.slice_in_dim(subband, 1, length, 2, along)
    odd_part = odd_part + LIFT_ALPHA * (even_part + forward_of(even_part, along))
    even_part = even_part + LIFT_BETA * (backward_of(odd_part, along) + odd_part)
    odd_part = odd_part + LIFT_GAMMA * (even_part + forward_of(even_part, along))
    even_part = even_part + LIFT_DELTA * (backward_of(odd_part, along) + odd_part)
    even_part = even_part / LIFT_KAPPA
    odd_part = odd_part * (LIFT_KAPPA / 2.0)
    return jnp.stack([even_part, odd_part], along + 1).reshape(subband.shape)


def lift_matrix(length):
    return lift_local(jnp.eye(length, dtype=jnp.float32), 0)


def apply_along(values, matrix, along):
    if along == 2:
        return jnp.dot(values, matrix.T, precision=HIGHEST)
    if along == 1:
        return jnp.einsum("wy,zyx->zwx", matrix, values, precision=HIGHEST)
    flat = values.reshape(values.shape[0], -1)
    result = jnp.dot(matrix, flat, precision=HIGHEST)
    return result.reshape((matrix.shape[0],) + values.shape[1:])


def mirror_edges(widened, along, devices, position):
    length = widened.shape[along] - 8
    middle = lax.slice_in_dim(widened, 4, 4 + length, 1, along)
    left_rim = jnp.where(
        position == 0,
        jnp.flip(lax.slice_in_dim(widened, 5, 9, 1, along), along),
        lax.slice_in_dim(widened, 0, 4, 1, along),
    )
    right_rim = jnp.where(
        position == devices - 1,
        jnp.flip(lax.slice_in_dim(widened, length - 1, length + 3, 1, along), along),
        lax.slice_in_dim(widened, length + 4, length + 8, 1, along),
    )
    return jnp.concatenate([left_rim, middle, right_rim], along)


def lift_plane(subband):
    rows_here = subband.shape[1]
    columns = subband.shape[2]
    extended = padded(subband, (("grp", 1), ("tile", 2)), 4)
    extended = mirror_edges(extended, 2, lax.axis_size("tile"), lax.axis_index("tile"))
    across = apply_along(extended, lift_matrix(columns + 8)[4 : 4 + columns], 2)
    across = mirror_edges(across, 1, lax.axis_size("grp"), lax.axis_index("grp"))
    return apply_along(across, lift_matrix(rows_here + 8)[4 : 4 + rows_here], 1)


def decompose(subband, level_index):
    subband = lift_plane(subband)
    subband = apply_along(subband, lift_matrix(subband.shape[0]), 0)
    if level_index + 1 < LEVELS:
        coarser = decompose(subband[::2, ::2, ::2], level_index + 1)
        subband = subband.at[::2, ::2, ::2].set(coarser)
    return subband


def body(quantized, scales):
    planes, rows_here, columns = quantized.shape
    blocks = quantized.astype(jnp.float32).reshape(planes, rows_here, columns // QB, QB)
    factor = jnp.transpose(scales, (1, 2, 0))[..., None]
    density = (blocks * factor).reshape(planes, rows_here, columns)
    return decompose(density, 0).astype(jnp.bfloat16)


def solution(mesh):
    return jax.shard_map(
        body,
        mesh=mesh,
        in_specs=(P(None, "grp", "tile"), P("tile", None, "grp")),
        out_specs=P(None, "grp", "tile"),
        check_vma=False,
    )
```

profile of v0, /device:TPU:320, one launch (start us, length us, event | category | flops | bytes accessed | tf_op | source)
XLA Modules:
  0.0 189.0 jit_solution(16697019599464206214)
XLA Ops:
  0.0 1.1 convert_multiply_fusion
  1.1 4.7 %collective-permute-start.1 = (f32[16,4,128]{2,1,0:T(4,128)S(1)}, f32[16,4,128]{2,1,0:T(4,128)S(1)}, u32[]{:S(2)}, u32[]{:S(2)}) collective-permute-start(f32[16,4,128]{2,1,0:T(4,128)S(1)} %get-tuple-element.36), channel_id=1, source_target_pairs={{64,0},{128,64},{192,128},{256,192},{320,256},{384,320},{448,384},... | collective-permute-start | bytes 98312 | tf_op jit(solution)/shard_map/ppermute | solution.py:26
  5.8 1.9 %collective-permute-start = (f32[16,4,128]{2,1,0:T(4,128)S(1)}, f32[16,4,128]{2,1,0:T(4,128)S(1)}, u32[]{:S(2)}, u32[]{:S(2)}) collective-permute-start(f32[16,4,128]{2,1,0:T(4,128)S(1)} %get-tuple-element.35), channel_id=1, source_target_pairs={{0,64},{64,128},{128,192},{192,256},{256,320},{320,384},{384,448},... | collective-permute-start | bytes 98312 | tf_op jit(solution)/shard_map/ppermute | solution.py:25
  8.0 1.3 slice.606
  9.3 1.3 slice.605
  12.6 0.6 copy-done.13
  13.3 0.5 copy-done.14
  13.9 0.6 multiply_bitcast_fusion.3
  14.8 0.6 copy-done.12
  15.5 0.5 copy-done.11
  16.2 0.6 multiply_bitcast_fusion.4
  16.8 0.6 fusion.174
  17.6 0.6 multiply_bitcast_fusion.6
  18.6 0.6 fusion.161
  19.3 0.6 fusion.150
  20.1 0.5 copy-done
  20.6 0.4 fusion.193
  21.1 2.7 %collective-permute-start.3 = (f32[16,56,4]{2,1,0:T(8,128)S(1)}, f32[16,56,4]{2,1,0:T(8,128)S(1)}, u32[]{:S(2)}, u32[]{:S(2)}) collective-permute-start(f32[16,56,4]{2,1,0:T(8,128)S(1)} %get-tuple-element.32), channel_id=1, source_target_pairs={{1,0},{2,1},{3,2},{4,3},{5,4},{6,5},{7,6},{8,7},{9,8},{10,9},{11,1... | collective-permute-start | bytes 43016 | tf_op jit(solution)/shard_map/ppermute | solution.py:26
  24.1 0.6 stack.139
  24.7 0.6 copy.81
  25.3 0.2 rev.55
  25.4 0.2 rev.54
  25.6 1.9 %collective-permute-start.2 = (f32[16,56,4]{2,1,0:T(8,128)S(1)}, f32[16,56,4]{2,1,0:T(8,128)S(1)}, u32[]{:S(2)}, u32[]{:S(2)}) collective-permute-start(f32[16,56,4]{2,1,0:T(8,128)S(1)} %get-tuple-element.31), channel_id=1, source_target_pairs={{0,1},{1,2},{2,3},{3,4},{4,5},{5,6},{6,7},{7,8},{8,9},{9,10},{10,1... | collective-permute-start | bytes 43016 | tf_op jit(solution)/shard_map/ppermute | solution.py:25
  27.5 4.3 %collective-permute-done.3 = f32[16,56,4]{2,1,0:T(8,128)S(1)} collective-permute-done((f32[16,56,4]{2,1,0:T(8,128)S(1)}, f32[16,56,4]{2,1,0:T(8,128)S(1)}, u32[]{:S(2)}, u32[]{:S(2)}) %collective-permute-start.3) | collective-permute-done | bytes 14368 | tf_op jit(solution)/shard_map/ppermute | solution.py:26
  31.9 12.2 %collective-permute-done.2 = f32[16,56,4]{2,1,0:T(8,128)S(1)} collective-permute-done((f32[16,56,4]{2,1,0:T(8,128)S(1)}, f32[16,56,4]{2,1,0:T(8,128)S(1)}, u32[]{:S(2)}, u32[]{:S(2)}) %collective-permute-start.2) | collective-permute-done | bytes 14368 | tf_op jit(solution)/shard_map/ppermute | solution.py:25
  44.2 1.1 fusion
  45.5 0.6 fusion.10
  46.1 0.5 fusion.16
  46.6 3.5 %slice.644 = f32[8,24,64]{2,0,1:T(8,128)S(1)} slice(f32[16,48,128]{2,0,1:T(8,128)S(1)} %fusion.16), slice={[0:16:2], [0:48:2], [0:128:2]} | slice | bytes 98304 | tf_op jit(solution)/shard_map/slice | solution.py:110
  50.2 3.4 %collective-permute-start.5 = (f32[8,4,64]{2,0,1:T(8,128)S(1)}, f32[8,4,64]{2,0,1:T(8,128)S(1)}, u32[]{:S(2)}, u32[]{:S(2)}) collective-permute-start(f32[8,4,64]{2,0,1:T(8,128)S(1)} %get-tuple-element.46), channel_id=1, source_target_pairs={{64,0},{128,64},{192,128},{256,192},{320,256},{384,320},{448,384},... | collective-permute-start | bytes 24584 | tf_op jit(solution)/shard_map/ppermute | solution.py:26
  53.6 2.4 %collective-permute-start.4 = (f32[8,4,64]{2,0,1:T(8,128)S(1)}, f32[8,4,64]{2,0,1:T(8,128)S(1)}, u32[]{:S(2)}, u32[]{:S(2)}) collective-permute-start(f32[8,4,64]{2,0,1:T(8,128)S(1)} %get-tuple-element.45), channel_id=1, source_target_pairs={{0,64},{64,128},{128,192},{192,256},{256,320},{320,384},{384,448},... | collective-permute-start | bytes 24584 | tf_op jit(solution)/shard_map/ppermute | solution.py:25
  56.1 5.3 %collective-permute-done.4 = f32[8,4,64]{2,0,1:T(8,128)S(1)} collective-permute-done((f32[8,4,64]{2,0,1:T(8,128)S(1)}, f32[8,4,64]{2,0,1:T(8,128)S(1)}, u32[]{:S(2)}, u32[]{:S(2)}) %collective-permute-start.4) | collective-permute-done | bytes 8224 | tf_op jit(solution)/shard_map/ppermute | solution.py:25
  61.4 0.2 fusion.196
  61.6 1.9 %collective-permute-start.7 = (f32[8,32,4]{2,0,1:T(8,128)S(1)}, f32[8,32,4]{2,0,1:T(8,128)S(1)}, u32[]{:S(2)}, u32[]{:S(2)}) collective-permute-start(f32[8,32,4]{2,0,1:T(8,128)S(1)} %get-tuple-element.42), channel_id=1, source_target_pairs={{1,0},{2,1},{3,2},{4,3},{5,4},{6,5},{7,6},{8,7},{9,8},{10,9},{11,1... | collective-permute-start | bytes 12296 | tf_op jit(solution)/shard_map/ppermute | solution.py:26
  63.8 2.4 %collective-permute-start.6 = (f32[8,32,4]{2,0,1:T(8,128)S(1)}, f32[8,32,4]{2,0,1:T(8,128)S(1)}, u32[]{:S(2)}, u32[]{:S(2)}) collective-permute-start(f32[8,32,4]{2,0,1:T(8,128)S(1)} %get-tuple-element.41), channel_id=1, source_target_pairs={{0,1},{1,2},{2,3},{3,4},{4,5},{5,6},{6,7},{7,8},{8,9},{9,10},{10,1... | collective-permute-start | bytes 12296 | tf_op jit(solution)/shard_map/ppermute | solution.py:25
  66.2 8.1 %collective-permute-done.6 = f32[8,32,4]{2,0,1:T(8,128)S(1)} collective-permute-done((f32[8,32,4]{2,0,1:T(8,128)S(1)}, f32[8,32,4]{2,0,1:T(8,128)S(1)}, u32[]{:S(2)}, u32[]{:S(2)}) %collective-permute-start.6) | collective-permute-done | bytes 4128 | tf_op jit(solution)/shard_map/ppermute | solution.py:25
  74.4 0.3 fusion.32
  74.8 0.2 convolution_bitcast_fusion
  75.3 0.2 fusion.34
  75.5 1.4 slice.686
  76.9 3.2 %collective-permute-start.9 = (f32[4,4,32]{2,0,1:T(4,128)S(1)}, f32[4,4,32]{2,0,1:T(4,128)S(1)}, u32[]{:S(2)}, u32[]{:S(2)}) collective-permute-start(f32[4,4,32]{2,0,1:T(4,128)S(1)} %get-tuple-element.56), channel_id=1, source_target_pairs={{64,0},{128,64},{192,128},{256,192},{320,256},{384,320},{448,384},... | collective-permute-start | bytes 6152 | tf_op jit(solution)/shard_map/ppermute | solution.py:26
  80.1 2.6 %collective-permute-start.8 = (f32[4,4,32]{2,0,1:T(4,128)S(1)}, f32[4,4,32]{2,0,1:T(4,128)S(1)}, u32[]{:S(2)}, u32[]{:S(2)}) collective-permute-start(f32[4,4,32]{2,0,1:T(4,128)S(1)} %get-tuple-element.55), channel_id=1, source_target_pairs={{0,64},{64,128},{128,192},{192,256},{256,320},{320,384},{384,448},... | collective-permute-start | bytes 6152 | tf_op jit(solution)/shard_map/ppermute | solution.py:25
  82.8 5.0 %collective-permute-done.8 = f32[4,4,32]{2,0,1:T(4,128)S(1)} collective-permute-done((f32[4,4,32]{2,0,1:T(4,128)S(1)}, f32[4,4,32]{2,0,1:T(4,128)S(1)}, u32[]{:S(2)}, u32[]{:S(2)}) %collective-permute-start.8) | collective-permute-done | bytes 2080 | tf_op jit(solution)/shard_map/ppermute | solution.py:25
  88.0 1.9 %collective-permute-start.11 = (f32[4,20,4]{2,0,1:T(4,128)S(1)}, f32[4,20,4]{2,0,1:T(4,128)S(1)}, u32[]{:S(2)}, u32[]{:S(2)}) collective-permute-start(f32[4,20,4]{2,0,1:T(4,128)S(1)} %get-tuple-element.52), channel_id=1, source_target_pairs={{1,0},{2,1},{3,2},{4,3},{5,4},{6,5},{7,6},{8,7},{9,8},{10,9},{11,1... | collective-permute-start | bytes 3848 | tf_op jit(solution)/shard_map/ppermute | solution.py:26
  90.2 2.4 %collective-permute-start.10 = (f32[4,20,4]{2,0,1:T(4,128)S(1)}, f32[4,20,4]{2,0,1:T(4,128)S(1)}, u32[]{:S(2)}, u32[]{:S(2)}) collective-permute-start(f32[4,20,4]{2,0,1:T(4,128)S(1)} %get-tuple-element.51), channel_id=1, source_target_pairs={{0,1},{1,2},{2,3},{3,4},{4,5},{5,6},{6,7},{7,8},{8,9},{9,10},{10,1... | collective-permute-start | bytes 3848 | tf_op jit(solution)/shard_map/ppermute | solution.py:25
  92.6 7.1 %collective-permute-done.10 = f32[4,20,4]{2,0,1:T(4,128)S(1)} collective-permute-done((f32[4,20,4]{2,0,1:T(4,128)S(1)}, f32[4,20,4]{2,0,1:T(4,128)S(1)}, u32[]{:S(2)}, u32[]{:S(2)}) %collective-permute-start.10) | collective-permute-done | bytes 1312 | tf_op jit(solution)/shard_map/ppermute | solution.py:25
  99.9 0.2 fusion.51
  100.1 0.2 convolution_bitcast_fusion.1
  100.5 0.2 fusion.55
  100.7 0.6 slice.724
  101.4 1.9 %collective-permute-start.13 = (f32[2,4,16]{2,0,1:T(2,128)S(1)}, f32[2,4,16]{2,0,1:T(2,128)S(1)}, u32[]{:S(2)}, u32[]{:S(2)}) collective-permute-start(f32[2,4,16]{2,0,1:T(2,128)S(1)} %get-tuple-element.64), channel_id=1, source_target_pairs={{64,0},{128,64},{192,128},{256,192},{320,256},{384,320},{448,384},... | collective-permute-start | bytes 1544 | tf_op jit(solution)/shard_map/ppermute | solution.py:26
  103.3 3.9 %collective-permute-start.12 = (f32[2,4,16]{2,0,1:T(2,128)S(1)}, f32[2,4,16]{2,0,1:T(2,128)S(1)}, u32[]{:S(2)}, u32[]{:S(2)}) collective-permute-start(f32[2,4,16]{2,0,1:T(2,128)S(1)} %get-tuple-element.63), channel_id=1, source_target_pairs={{0,64},{64,128},{128,192},{192,256},{256,320},{320,384},{384,448},... | collective-permute-start | bytes 1544 | tf_op jit(solution)/shard_map/ppermute | solution.py:25
  107.5 3.4 %collective-permute-done.12 = f32[2,4,16]{2,0,1:T(2,128)S(1)} collective-permute-done((f32[2,4,16]{2,0,1:T(2,128)S(1)}, f32[2,4,16]{2,0,1:T(2,128)S(1)}, u32[]{:S(2)}, u32[]{:S(2)}) %collective-permute-start.12) | collective-permute-done | bytes 544 | tf_op jit(solution)/shard_map/ppermute | solution.py:25
  111.0 1.9 %collective-permute-start.15 = (f32[2,14,4]{2,0,1:T(2,128)S(1)}, f32[2,14,4]{2,0,1:T(2,128)S(1)}, u32[]{:S(2)}, u32[]{:S(2)}) collective-permute-start(f32[2,14,4]{2,0,1:T(2,128)S(1)} %get-tuple-element.60), channel_id=1, source_target_pairs={{1,0},{2,1},{3,2},{4,3},{5,4},{6,5},{7,6},{8,7},{9,8},{10,9},{11,1... | collective-permute-start | bytes 1352 | tf_op jit(solution)/shard_map/ppermute | solution.py:26
  113.4 2.6 %collective-permute-start.14 = (f32[2,14,4]{2,0,1:T(2,128)S(1)}, f32[2,14,4]{2,0,1:T(2,128)S(1)}, u32[]{:S(2)}, u32[]{:S(2)}) collective-permute-start(f32[2,14,4]{2,0,1:T(2,128)S(1)} %get-tuple-element.59), channel_id=1, source_target_pairs={{0,1},{1,2},{2,3},{3,4},{4,5},{5,6},{6,7},{7,8},{8,9},{9,10},{10,1... | collective-permute-start | bytes 1352 | tf_op jit(solution)/shard_map/ppermute | solution.py:25
  116.0 6.6 %collective-permute-done.14 = f32[2,14,4]{2,0,1:T(2,128)S(1)} collective-permute-done((f32[2,14,4]{2,0,1:T(2,128)S(1)}, f32[2,14,4]{2,0,1:T(2,128)S(1)}, u32[]{:S(2)}, u32[]{:S(2)}) %collective-permute-start.14) | collective-permute-done | bytes 480 | tf_op jit(solution)/shard_map/ppermute | solution.py:25
  122.8 0.1 fusion.83
  123.0 0.1 convolution_bitcast_fusion.2
  123.3 0.7 copy-done.9
  124.0 0.2 fusion.129
  124.2 12.2 %scatter_fusion = f32[4,12,32]{2,0,1:T(4,128)S(1)} fusion(f32[4,12,32]{2,0,1:T(4,128)S(1)} %fusion.55, s32[192]{0:T(256)S(1)} %reshape.72, f32[192]{0:T(256)S(1)} %reshape.74), kind=kCustom, calls=%fused_computation | custom fusion | bytes 4608 | tf_op jit(solution)/shard_map/scatter | solution.py:111
  136.5 6.2 %scatter_fusion.1 = f32[12288]{0:T(1024)S(1)} fusion(f32[12288]{0:T(1024)S(1)} %reshape.64, s32[1536]{0:T(1024)S(1)} %reshape.78, f32[1536]{0:T(1024)S(1)} %reshape.80), kind=kCustom, calls=%fused_computation.1 | custom fusion | bytes 24576 | tf_op jit(solution)/shard_map/scatter | solution.py:111
  142.7 45.6 %scatter_fusion.2 = f32[98304]{0:T(1024)S(1)} fusion(f32[98304]{0:T(1024)S(1)} %bitcast.141, s32[12288]{0:T(1024)S(1)} %reshape.84, f32[12288]{0:T(1024)S(1)} %scatter_fusion.1), kind=kCustom, calls=%fused_computation.2 | custom fusion | bytes 196608
  188.3 0.7 convert_element_type.146
  (280 shorter events, 6.4 us)
Async XLA Ops:
  1.1 18.9 %collective-permute-start.1 = (f32[16,4,128]{2,1,0:T(4,128)S(1)}, f32[16,4,128]{2,1,0:T(4,128)S(1)}, u32[]{:S(2)}, u32[]{:S(2)}) collective-permute-start(f32[16,4,128]{2,1,0:T(4,128)S(1)} %get-tuple-element.36), channel_id=1, source_target_pairs={{64,0},{128,64},{192,128},{256,192},{320,256},{384,320},{448,384},... | collective-permute-start | bytes 98312 | tf_op jit(solution)/shard_map/ppermute | solution.py:26
  5.8 14.2 %collective-permute-start = (f32[16,4,128]{2,1,0:T(4,128)S(1)}, f32[16,4,128]{2,1,0:T(4,128)S(1)}, u32[]{:S(2)}, u32[]{:S(2)}) collective-permute-start(f32[16,4,128]{2,1,0:T(4,128)S(1)} %get-tuple-element.35), channel_id=1, source_target_pairs={{0,64},{64,128},{128,192},{192,256},{256,320},{320,384},{384,448},... | collective-permute-start | bytes 98312 | tf_op jit(solution)/shard_map/ppermute | solution.py:25
  12.5 0.7 copy-start.13
  13.2 0.7 copy-start.14
  14.7 0.7 copy-start.12
  15.4 0.7 copy-start.11
  20.0 0.6 copy-start
  21.1 10.8 %collective-permute-start.3 = (f32[16,56,4]{2,1,0:T(8,128)S(1)}, f32[16,56,4]{2,1,0:T(8,128)S(1)}, u32[]{:S(2)}, u32[]{:S(2)}) collective-permute-start(f32[16,56,4]{2,1,0:T(8,128)S(1)} %get-tuple-element.32), channel_id=1, source_target_pairs={{1,0},{2,1},{3,2},{4,3},{5,4},{6,5},{7,6},{8,7},{9,8},{10,9},{11,1... | collective-permute-start | bytes 43016 | tf_op jit(solution)/shard_map/ppermute | solution.py:26
  25.6 18.5 %collective-permute-start.2 = (f32[16,56,4]{2,1,0:T(8,128)S(1)}, f32[16,56,4]{2,1,0:T(8,128)S(1)}, u32[]{:S(2)}, u32[]{:S(2)}) collective-permute-start(f32[16,56,4]{2,1,0:T(8,128)S(1)} %get-tuple-element.31), channel_id=1, source_target_pairs={{0,1},{1,2},{2,3},{3,4},{4,5},{5,6},{6,7},{7,8},{8,9},{9,10},{10,1... | collective-permute-start | bytes 43016 | tf_op jit(solution)/shard_map/ppermute | solution.py:25
  31.9 12.3 %copy-start.1 = (f32[16,4,128]{2,1,0:T(4,128)S(1)}, f32[16,4,128]{2,1,0:T(4,128)}, u32[]{:S(2)}) copy-start(f32[16,4,128]{2,1,0:T(4,128)} %copy-done) | copy-start | bytes 98308
  50.2 5.9 %copy-start.2 = (f32[12,1,24]{2,1,0:T(1,128)S(1)}, f32[12,1,24]{2,1,0:T(1,128)}, u32[]{:S(2)}) copy-start(f32[12,1,24]{2,1,0:T(1,128)} %stack.139) | copy-start | bytes 3460
  50.2 5.9 %copy-start.3 = (f32[12,1,24]{2,1,0:T(1,128)S(1)}, f32[12,1,24]{2,1,0:T(1,128)}, u32[]{:S(2)}) copy-start(f32[12,1,24]{2,1,0:T(1,128)} %copy.81) | copy-start | bytes 3460
  50.2 5.9 %collective-permute-start.5 = (f32[8,4,64]{2,0,1:T(8,128)S(1)}, f32[8,4,64]{2,0,1:T(8,128)S(1)}, u32[]{:S(2)}, u32[]{:S(2)}) collective-permute-start(f32[8,4,64]{2,0,1:T(8,128)S(1)} %get-tuple-element.46), channel_id=1, source_target_pairs={{64,0},{128,64},{192,128},{256,192},{320,256},{384,320},{448,384},... | collective-permute-start | bytes 24584 | tf_op jit(solution)/shard_map/ppermute | solution.py:26
  53.6 7.7 %collective-permute-start.4 = (f32[8,4,64]{2,0,1:T(8,128)S(1)}, f32[8,4,64]{2,0,1:T(8,128)S(1)}, u32[]{:S(2)}, u32[]{:S(2)}) collective-permute-start(f32[8,4,64]{2,0,1:T(8,128)S(1)} %get-tuple-element.45), channel_id=1, source_target_pairs={{0,64},{64,128},{128,192},{192,256},{256,320},{320,384},{384,448},... | collective-permute-start | bytes 24584 | tf_op jit(solution)/shard_map/ppermute | solution.py:25
  61.4 2.1 %copy-start.6 = (f32[4,1,8]{2,0,1:T(4,128)S(1)}, f32[4,1,8]{2,0,1:T(4,128)}, u32[]{:S(2)}) copy-start(f32[4,1,8]{2,0,1:T(4,128)} %get-tuple-element.19) | copy-start | bytes 388
  61.6 2.0 %copy-start.5 = (f32[4,1,8]{2,0,1:T(4,128)S(1)}, f32[4,1,8]{2,0,1:T(4,128)}, u32[]{:S(2)}) copy-start(f32[4,1,8]{2,0,1:T(4,128)} %fusion.161) | copy-start | bytes 388
  61.6 4.6 %collective-permute-start.7 = (f32[8,32,4]{2,0,1:T(8,128)S(1)}, f32[8,32,4]{2,0,1:T(8,128)S(1)}, u32[]{:S(2)}, u32[]{:S(2)}) collective-permute-start(f32[8,32,4]{2,0,1:T(8,128)S(1)} %get-tuple-element.42), channel_id=1, source_target_pairs={{1,0},{2,1},{3,2},{4,3},{5,4},{6,5},{7,6},{8,7},{9,8},{10,9},{11,1... | collective-permute-start | bytes 12296 | tf_op jit(solution)/shard_map/ppermute | solution.py:26
  63.8 10.5 %collective-permute-start.6 = (f32[8,32,4]{2,0,1:T(8,128)S(1)}, f32[8,32,4]{2,0,1:T(8,128)S(1)}, u32[]{:S(2)}, u32[]{:S(2)}) collective-permute-start(f32[8,32,4]{2,0,1:T(8,128)S(1)} %get-tuple-element.41), channel_id=1, source_target_pairs={{0,1},{1,2},{2,3},{3,4},{4,5},{5,6},{6,7},{7,8},{8,9},{9,10},{10,1... | collective-permute-start | bytes 12296 | tf_op jit(solution)/shard_map/ppermute | solution.py:25
  76.9 5.9 %collective-permute-start.9 = (f32[4,4,32]{2,0,1:T(4,128)S(1)}, f32[4,4,32]{2,0,1:T(4,128)S(1)}, u32[]{:S(2)}, u32[]{:S(2)}) collective-permute-start(f32[4,4,32]{2,0,1:T(4,128)S(1)} %get-tuple-element.56), channel_id=1, source_target_pairs={{64,0},{128,64},{192,128},{256,192},{320,256},{384,320},{448,384},... | collective-permute-start | bytes 6152 | tf_op jit(solution)/shard_map/ppermute | solution.py:26
  80.1 7.7 %collective-permute-start.8 = (f32[4,4,32]{2,0,1:T(4,128)S(1)}, f32[4,4,32]{2,0,1:T(4,128)S(1)}, u32[]{:S(2)}, u32[]{:S(2)}) collective-permute-start(f32[4,4,32]{2,0,1:T(4,128)S(1)} %get-tuple-element.55), channel_id=1, source_target_pairs={{0,64},{64,128},{128,192},{192,256},{256,320},{320,384},{384,448},... | collective-permute-start | bytes 6152 | tf_op jit(solution)/shard_map/ppermute | solution.py:25
  87.9 2.0 %copy-start.8 = (f32[2,1,4]{2,0,1:T(2,128)S(1)}, f32[2,1,4]{2,0,1:T(2,128)}, u32[]{:S(2)}) copy-start(f32[2,1,4]{2,0,1:T(2,128)} %get-tuple-element.13) | copy-start | bytes 100
  87.9 2.0 %copy-start.7 = (f32[2,1,4]{2,0,1:T(2,128)S(1)}, f32[2,1,4]{2,0,1:T(2,128)}, u32[]{:S(2)}) copy-start(f32[2,1,4]{2,0,1:T(2,128)} %fusion.174) | copy-start | bytes 100
  88.0 4.7 %collective-permute-start.11 = (f32[4,20,4]{2,0,1:T(4,128)S(1)}, f32[4,20,4]{2,0,1:T(4,128)S(1)}, u32[]{:S(2)}, u32[]{:S(2)}) collective-permute-start(f32[4,20,4]{2,0,1:T(4,128)S(1)} %get-tuple-element.52), channel_id=1, source_target_pairs={{1,0},{2,1},{3,2},{4,3},{5,4},{6,5},{7,6},{8,7},{9,8},{10,9},{11,1... | collective-permute-start | bytes 3848 | tf_op jit(solution)/shard_map/ppermute | solution.py:26
  90.2 9.5 %collective-permute-start.10 = (f32[4,20,4]{2,0,1:T(4,128)S(1)}, f32[4,20,4]{2,0,1:T(4,128)S(1)}, u32[]{:S(2)}, u32[]{:S(2)}) collective-permute-start(f32[4,20,4]{2,0,1:T(4,128)S(1)} %get-tuple-element.51), channel_id=1, source_target_pairs={{0,1},{1,2},{2,3},{3,4},{4,5},{5,6},{6,7},{7,8},{8,9},{9,10},{10,1... | collective-permute-start | bytes 3848 | tf_op jit(solution)/shard_map/ppermute | solution.py:25
  101.3 5.9 %copy-start.4 = (f32[7,1,14]{2,0,1:T(8,128)S(1)}, f32[7,1,14]{2,0,1:T(8,128)}, u32[]{:S(2)}) copy-start(f32[7,1,14]{2,0,1:T(8,128)} %fusion.150) | copy-start | bytes 1180
  101.4 6.1 %collective-permute-start.13 = (f32[2,4,16]{2,0,1:T(2,128)S(1)}, f32[2,4,16]{2,0,1:T(2,128)S(1)}, u32[]{:S(2)}, u32[]{:S(2)}) collective-permute-start(f32[2,4,16]{2,0,1:T(2,128)S(1)} %get-tuple-element.64), channel_id=1, source_target_pairs={{64,0},{128,64},{192,128},{256,192},{320,256},{384,320},{448,384},... | collective-permute-start | bytes 1544 | tf_op jit(solution)/shard_map/ppermute | solution.py:26
  103.3 7.6 %collective-permute-start.12 = (f32[2,4,16]{2,0,1:T(2,128)S(1)}, f32[2,4,16]{2,0,1:T(2,128)S(1)}, u32[]{:S(2)}, u32[]{:S(2)}) collective-permute-start(f32[2,4,16]{2,0,1:T(2,128)S(1)} %get-tuple-element.63), channel_id=1, source_target_pairs={{0,64},{64,128},{128,192},{192,256},{256,320},{320,384},{384,448},... | collective-permute-start | bytes 1544 | tf_op jit(solution)/shard_map/ppermute | solution.py:25
  111.0 5.0 %collective-permute-start.15 = (f32[2,14,4]{2,0,1:T(2,128)S(1)}, f32[2,14,4]{2,0,1:T(2,128)S(1)}, u32[]{:S(2)}, u32[]{:S(2)}) collective-permute-start(f32[2,14,4]{2,0,1:T(2,128)S(1)} %get-tuple-element.60), channel_id=1, source_target_pairs={{1,0},{2,1},{3,2},{4,3},{5,4},{6,5},{7,6},{8,7},{9,8},{10,9},{11,1... | collective-permute-start | bytes 1352 | tf_op jit(solution)/shard_map/ppermute | solution.py:26
  113.4 9.3 %collective-permute-start.14 = (f32[2,14,4]{2,0,1:T(2,128)S(1)}, f32[2,14,4]{2,0,1:T(2,128)S(1)}, u32[]{:S(2)}, u32[]{:S(2)}) collective-permute-start(f32[2,14,4]{2,0,1:T(2,128)S(1)} %get-tuple-element.59), channel_id=1, source_target_pairs={{0,1},{1,2},{2,3},{3,4},{4,5},{5,6},{6,7},{7,8},{8,9},{9,10},{10,1... | collective-permute-start | bytes 1352 | tf_op jit(solution)/shard_map/ppermute | solution.py:25
  123.3 0.7 copy-start.9
  123.3 0.7 copy-start.10
where the time goes:
time: 190 us; the launch traced here: 189 us
  local copies, waits for them, and re-layouts  81.6 us (43%)
  waiting for transfers between devices  52 us (27%)
  starting transfers between devices  41.9 us (22%)
  other arithmetic  7.8 us (4%)
  matrix products  3.92 us (2%)
    unnamed x35, local copies, waits for them, and re-layouts  49.3 us
    ppermute x8, waiting for transfers between devices, padded(): before = lax.ppermute(last, axis, up)  47.7 us
    ppermute x8, starting transfers between devices, padded(): after = lax.ppermute(initial, axis, down)  21.7 us
    ppermute x8, starting transfers between devices, padded(): before = lax.ppermute(last, axis, up)  20.2 us
    scatter x4, local copies, waits for them, and re-layouts, decompose(): subband = subband.at[::2, ::2, ::2].set(coarser)  18.5 us
    slice x3, local copies, waits for them, and re-layouts, decompose(): coarser = decompose(subband[::2, ::2, ::2], level_index + 1)  5.59 us
    ppermute x8, waiting for transfers between devices, padded(): after = lax.ppermute(initial, axis, down)  4.31 us
    another operation x27, other arithmetic, lift_local(): return jnp.stack([even_part, odd_part], along + 1).reshape(subband.shape)  4.12 us
  transfers between devices with their start and end apart: 16, of which 8 were waited for; matrix products, arithmetic and copies ran while one was open for 6% of the time, Pallas kernels for 0%

commit v1 on v0

v1 whole, which is shorter than its diff:
```python
import functools

import jax
import jax.numpy as jnp
import numpy as np
from jax import lax
from jax.experimental import pallas as pl
from jax.experimental.pallas import tpu as pltpu
from jax.sharding import PartitionSpec as P

LEVELS = 4
ALPHA = -1.586134342059924
BETA = -0.052980118572961
GAMMA = 0.882911075530934
DELTA = 0.443506852043971
KAPPA = 1.230174104914001

NZ, BY, BX = 16, 48, 128
OFF = (0, 16, 24, 28)
NP = 30
SR = (0, 0, 1, 3)
SL = (0, 1, 2, 0)
MESH = pl.DeviceIdType.MESH
F32, BF16 = jnp.float32, jnp.bfloat16


def lift_list(v):
    e, o = list(v[0::2]), list(v[1::2])
    m = len(e)
    up = lambda s: [s[min(i + 1, m - 1)] for i in range(m)]
    down = lambda s: [s[max(i - 1, 0)] for i in range(m)]
    o = [x + ALPHA * (a + b) for x, a, b in zip(o, e, up(e))]
    e = [x + BETA * (a + b) for x, a, b in zip(e, down(o), o)]
    o = [x + GAMMA * (a + b) for x, a, b in zip(o, e, up(e))]
    e = [x + DELTA * (a + b) for x, a, b in zip(e, down(o), o)]
    e = [x * (1.0 / KAPPA) for x in e]
    o = [x * (KAPPA / 2.0) for x in o]
    return [x for pair in zip(e, o) for x in pair]


def level_matrices(n):
    low, out = np.eye(n), []
    for _ in range(LEVELS):
        full = np.stack(lift_list(list(low)))
        out.append(full)
        low = full[::2]
    return out


def split(a):
    hi = a.astype(np.float32).astype(BF16)
    lo = (a - hi.astype(np.float64)).astype(np.float32).astype(BF16)
    return hi, lo


@functools.cache
def x_matrices():
    w = level_matrices(3 * BX)
    m = np.zeros((3, LEVELS, BX, 2 * BX))
    for v in range(3):
        for l in range(LEVELS):
            b, win = BX >> l, 8 << l
            mine = w[l][:, v * BX : (v + 1) * BX]
            for j in range(b):
                m[v, l, :, j << l] = mine[v * b + j]
            for start in range(0, BX, win):
                if v < 2:
                    for j in range(4 if l == 0 else 7):
                        lane = start + (j << l) + SR[l]
                        if j << l < win:
                            m[v, l, :, BX + lane] = mine[(v + 1) * b + j]
                if v > 0:
                    for j in range(1, 5 if l == 0 else 7):
                        lane = (start - (j << l) + SL[l]) % BX
                        m[v, l, :, BX + lane] = mine[v * b - j]
    hi, lo = split(m)
    return np.concatenate([hi, lo], axis=2)


@functools.cache
def y_matrices(groups):
    n = groups * BY
    w = level_matrices(n)
    m = np.zeros((groups, LEVELS, BY + 16, BY))
    for g in range(groups):
        for l in range(LEVELS):
            b = BY >> l
            mine = w[l][:, g * BY : (g + 1) * BY]
            for j in range(b):
                m[g, l, j << l] = mine[g * b + j]
            for k in range(8):
                r = (g + 1) * b + k
                if r < n >> l:
                    m[g, l, BY + k] = mine[r]
                r = g * b - 8 + k
                if r >= max((g - 1) * b, 0):
                    m[g, l, BY + 8 + k] = mine[r]
    hi, lo = split(m)
    return np.concatenate([hi, hi, lo], axis=3)


def hilo(x):
    hi = x.astype(BF16)
    return hi, (x - hi.astype(F32)).astype(BF16)


def stacked(x):
    hi, lo = hilo(x)
    return jnp.concatenate([hi, lo, hi], axis=0)


def dot(a, b):
    return jnp.dot(a, b, preferred_element_type=F32)


def lanes_of(shape):
    return lax.broadcasted_iota(jnp.int32, shape, len(shape) - 1)


def kernel(
    groups, tiles,
    q_hbm, s_hbm, mx_hbm, ay_hbm, out_ref,
    qv, sv, mxv, ayv, zh, zl, pk, from_left, from_right, yo,
    send0, send1, recv0, recv1, recv2,
    load_sem, xs_sem, xr_sem, ys_sem, yr_sem,
):
    g, t = lax.axis_index("grp"), lax.axis_index("tile")
    right, left = lax.rem(t + 1, tiles), lax.rem(t + tiles - 1, tiles)
    below, above = lax.rem(g + 1, groups), lax.rem(g + groups - 1, groups)
    below2, above2 = lax.rem(g + 2, groups), lax.rem(g + groups - 2, groups)

    barrier = pltpu.get_barrier_semaphore()
    for dev in ((g, left), (g, right), (above, t), (below, t), (above2, t), (below2, t)):
        pl.semaphore_signal(barrier, inc=1, device_id=dev, device_id_type=MESH)

    side = jnp.where(t == 0, 0, jnp.where(t == tiles - 1, 2, 1))
    loads = [
        pltpu.make_async_copy(q_hbm, qv, load_sem.at[0]),
        pltpu.make_async_copy(s_hbm, sv, load_sem.at[1]),
        pltpu.make_async_copy(mx_hbm.at[side], mxv, load_sem.at[2]),
        pltpu.make_async_copy(ay_hbm.at[g], ayv, load_sem.at[3]),
    ]
    for c in loads:
        c.start()
    loads[1].wait()
    loads[0].wait()

    st = jnp.transpose(sv[0])
    for c in range(3):
        rows = slice(16 * c, 16 * c + 16)
        band = [qv[z, rows, :].astype(F32) * st[rows, z : z + 1] for z in range(NZ)]
        for l in range(LEVELS):
            band = lift_list(band)
            for p, v in enumerate(band):
                hi, lo = hilo(v)
                zh[OFF[l] + p, rows, :] = hi
                zl[OFF[l] + p, rows, :] = lo
            band = band[0::2]

    loads[2].wait()
    own, packs = [], []
    lane = lanes_of((1, 1, BX))
    for l in range(LEVELS):
        n, win = NZ >> l, 8 << l
        h = zh[OFF[l] : OFF[l] + n].reshape(n * BY, BX)
        low = zl[OFF[l] : OFF[l] + n].reshape(n * BY, BX)
        mh, ml = mxv[l, :BX], mxv[l, BX:]
        r = dot(jnp.concatenate([h, low, h], axis=1), jnp.concatenate([mh, mh, ml], axis=0))
        own.append(r[:, :BX].reshape(n, BY, BX))
        if l == 0:
            plane = ((lane + 4) // 8) % NZ
        else:
            to_right = (lane % (1 << l)) == SR[l] % (1 << l)
            plane = jnp.where(to_right, lane // win, (lane // win + 1) % n)
        which = lax.broadcasted_iota(jnp.int32, (n, 1, BX), 0)
        packs.append(jnp.sum(jnp.where(which == plane, r[:, BX:].reshape(n, BY, BX), 0.0), axis=0))
    lane = lanes_of((BY, BX))
    pk[0] = jnp.where(lane % 2 == 0, packs[1], jnp.where(lane % 4 == 1, packs[2], packs[3]))
    pk[1] = packs[0]
    pk[2] = jnp.where(lane % 2 == 1, packs[1], jnp.where(lane % 4 == 2, packs[2], packs[3]))

    def remote(src, dst, ss, rs, dev):
        return pltpu.make_async_remote_copy(
            src_ref=src, dst_ref=dst, send_sem=ss, recv_sem=rs, device_id=dev, device_id_type=MESH
        )

    pl.semaphore_wait(barrier, 6)
    xcopies = [
        remote(pk.at[0:2], from_left, xs_sem.at[0], xr_sem.at[0], (g, right)),
        remote(pk.at[1:3], from_right, xs_sem.at[1], xr_sem.at[1], (g, left)),
    ]
    for c in xcopies:
        c.start()

    loads[3].wait()
    for l in range(LEVELS):
        n = NZ >> l
        r = dot(ayv[l], stacked(jnp.concatenate([own[l][p] for p in range(n)], axis=1)))
        for p in range(n):
            yo[OFF[l] + p] = r[:, p * BX : (p + 1) * BX]

    for c in xcopies:
        c.wait()
    edge0 = dot(
        ayv[0], stacked(jnp.where(lane % 8 < 4, from_left[1], from_right[0]))
    )
    edges = dot(
        ayv[1:].reshape(3 * (BY + 16), 3 * BY),
        stacked(jnp.concatenate([from_left[0], from_right[1]], axis=1)),
    )

    def edge_of(l, p, rows):
        n = rows.stop - rows.start
        lane = lanes_of((n, BX))
        win = 8 << l
        turned = lambda e, s: pltpu.roll(e, (-s) % BX, 1)
        if l == 0:
            return jnp.where((lane + 4) % BX < 8, turned(edge0[rows], 8 * p), 0.0)
        base = (l - 1) * (BY + 16)
        e = edges[base + rows.start : base + rows.stop]
        a = turned(e[:, :BX], win * p + SR[l])
        b = turned(e[:, BX:], win * p + SL[l])
        return jnp.where(lane < win, a, 0.0) + jnp.where(lane >= BX - win, b, 0.0)

    tail = slice(BY, BY + 16)
    for l in range(LEVELS):
        for p in range(NZ >> l):
            r = yo[OFF[l] + p, BY:, :] + edge_of(l, p, tail)
            if l == 0:
                send0[0, p] = r[0:4]
                send0[1, p] = r[12:16]
            else:
                send1[0, OFF[l] - NZ + p] = r[0:8]
                send1[1, OFF[l] - NZ + p] = r[8:16]
    ycopies = [
        remote(send0.at[0], recv0.at[0], ys_sem.at[0], yr_sem.at[0], (below, t)),
        remote(send0.at[1], recv0.at[1], ys_sem.at[1], yr_sem.at[1], (above, t)),
        remote(send1.at[0], recv1.at[0], ys_sem.at[2], yr_sem.at[2], (below, t)),
        remote(send1.at[1], recv1.at[1], ys_sem.at[3], yr_sem.at[3], (above, t)),
        remote(send1.at[0, 12:14], recv2, ys_sem.at[4], yr_sem.at[4], (below2, t)),
    ]
    for c in ycopies:
        c.start()

    row = lax.broadcasted_iota(jnp.int32, (BY, BX), 0)
    here = slice(0, BY)
    for z in range(NZ):
        value = None
        for l in reversed(range(LEVELS)):
            if z % (1 << l):
                continue
            p = z >> l
            part = yo[OFF[l] + p, :BY, :] + edge_of(l, p, here)
            if value is None:
                value = part
            else:
                step = 2 << l
                value = jnp.where((row % step == 0) & (lane % step == 0), value, part)
        yo[z, :BY, :] = value

    for c in ycopies:
        c.wait()
    lane = lanes_of((1, BX))

    def valid(l, p, j, v):
        if l and p % 2 == 0 and j % 2 == 0 and l < LEVELS - 1:
            return jnp.where(lane % (2 << l) == 1 << l, v, 0.0)
        if l:
            return jnp.where(lane % (1 << l) == 0, v, 0.0)
        if p % 2 == 0 and j % 2 == 0:
            return jnp.where(lane % 2 == 1, v, 0.0)
        return v

    for z in range(NZ):
        adds = {}
        for l in range(LEVELS):
            if z % (1 << l):
                continue
            p = z >> l
            for k in range(3 if l == 0 else 7):
                if k << l < BY:
                    v = recv0[0, p, k : k + 1, :] if l == 0 else recv1[0, OFF[l] - NZ + p, k : k + 1, :]
                    adds.setdefault(k << l, []).append(valid(l, p, k, v))
            for k in range(4 if l == 0 else 2, 8):
                r = BY - ((8 - k) << l)
                v = recv0[1, p, k - 4 : k - 3, :] if l == 0 else recv1[1, OFF[l] - NZ + p, k : k + 1, :]
                adds.setdefault(r, []).append(valid(l, p, k, v))
            if l == 3:
                adds[0].append(valid(l, p, 6, recv2[p, 6:7, :]))
        for r, vs in adds.items():
            yo[z, r : r + 1, :] = functools.reduce(lambda a, b: a + b, vs, yo[z, r : r + 1, :])
        out_ref[z] = yo[z, :BY, :].astype(BF16)


def body(quantized, scales):
    groups, tiles = lax.axis_size("grp"), lax.axis_size("tile")
    hbm = pl.BlockSpec(memory_space=pl.ANY)
    dma = pltpu.SemaphoreType.DMA
    return pl.pallas_call(
        functools.partial(kernel, groups, tiles),
        out_shape=jax.ShapeDtypeStruct((NZ, BY, BX), BF16),
        in_specs=[hbm] * 4,
        out_specs=pl.BlockSpec(memory_space=pltpu.VMEM),
        scratch_shapes=[
            pltpu.VMEM((NZ, BY, BX), BF16),
            pltpu.VMEM((1, NZ, BY), F32),
            pltpu.VMEM((LEVELS, 2 * BX, 2 * BX), BF16),
            pltpu.VMEM((LEVELS, BY + 16, 3 * BY), BF16),
            pltpu.VMEM((NP, BY, BX), BF16),
            pltpu.VMEM((NP, BY, BX), BF16),
            pltpu.VMEM((3, BY, BX), F32),
            pltpu.VMEM((2, BY, BX), F32),
            pltpu.VMEM((2, BY, BX), F32),
            pltpu.VMEM((NP, BY + 16, BX), F32),
            pltpu.VMEM((2, NZ, 4, BX), F32),
            pltpu.VMEM((2, NP - NZ, 8, BX), F32),
            pltpu.VMEM((2, NZ, 4, BX), F32),
            pltpu.VMEM((2, NP - NZ, 8, BX), F32),
            pltpu.VMEM((2, 8, BX), F32),
            dma((4,)), dma((2,)), dma((2,)), dma((5,)), dma((5,)),
        ],
        compiler_params=pltpu.CompilerParams(collective_id=0, has_side_effects=True),
    )(quantized, scales, jnp.asarray(x_matrices()), jnp.asarray(y_matrices(groups)))


def solution(mesh):
    return jax.shard_map(
        body,
        mesh=mesh,
        in_specs=(P(None, "grp", "tile"), P("tile", None, "grp")),
        out_specs=P(None, "grp", "tile"),
        check_vma=False,
    )
```

time: 190 us -> 25 us (0.13)
  the two profiles are of different devices: /device:TPU:320 before, /device:TPU:2 now
where the time goes in v1:
time: 25 us; the launch traced here: 24.9 us
  Pallas kernels  23.2 us (93%)
  local copies, waits for them, and re-layouts  1.62 us (6%)
    pallas_call x1, Pallas kernels, body(): pl.pallas_call(functools.partial(kernel, groups, tiles), out_shape=jax.Sh...  23.2 us
    unnamed x1, local copies, waits for them, and re-layouts  1.62 us

profile of v1, /device:TPU:2, one launch (start us, length us, event | category | flops | bytes accessed | tf_op | source)
XLA Modules:
  0.0 24.9 jit_solution(8687568222519563862)
XLA Ops:
  0.0 23.2 %shard_map.46 = bf16[16,48,128]{2,1,0:T(8,128)(2,1)} custom-call(bf16[16,48,128]{2,1,0:T(8,128)(2,1)} %q_hbm.1, f32[1,16,48]{2,1,0:T(8,128)} %s_hbm.1, bf16[3,4,256,256]{3,2,1,0:T(8,128)(2,1)} %constant.4.clone.mx_hbm, bf16[8,4,64,144]{3,2,1,0:T(8,128)(2,1)} %constant.5.clone.ay_hbm), custom_call_target="tpu_custom_call" | custom-call | tf_op jit(solution)/shard_map/pallas_call | solution.py:299
  23.3 1.6 %copy.6 = bf16[16,48,128]{2,1,0:T(8,128)(2,1)} copy(bf16[16,48,128]{2,1,0:T(8,128)(2,1)} %shard_map.46) | data formatting | bytes 393216

commit v2 on v1

--- a/solution.py
+++ b/solution.py
@@ -129,9 +129,18 @@
     below, above = lax.rem(g + 1, groups), lax.rem(g + groups - 1, groups)
     below2, above2 = lax.rem(g + 2, groups), lax.rem(g + groups - 2, groups)
 
+    has_left, has_right = t > 0, t < tiles - 1
+    has_above, has_below = g > 0, g < groups - 1
+    has_above2, has_below2 = g > 1, g < groups - 2
     barrier = pltpu.get_barrier_semaphore()
-    for dev in ((g, left), (g, right), (above, t), (below, t), (above2, t), (below2, t)):
-        pl.semaphore_signal(barrier, inc=1, device_id=dev, device_id_type=MESH)
+    for there, dev in (
+        (has_left, (g, left)), (has_right, (g, right)),
+        (has_above, (above, t)), (has_below, (below, t)),
+        (has_above2, (above2, t)), (has_below2, (below2, t)),
+    ):
+        @pl.when(there)
+        def _():
+            pl.semaphore_signal(barrier, inc=1, device_id=dev, device_id_type=MESH)
 
     side = jnp.where(t == 0, 0, jnp.where(t == tiles - 1, 2, 1))
     loads = [
@@ -142,6 +151,15 @@
     ]
     for c in loads:
         c.start()
+    for there, buffers in (
+        (has_left, (from_left,)), (has_right, (from_right,)),
+        (has_above, (recv0.at[0], recv1.at[0])), (has_below, (recv0.at[1], recv1.at[1])),
+        (has_above2, (recv2,)),
+    ):
+        @pl.when(jnp.logical_not(there))
+        def _():
+            for b in buffers:
+                b[...] = jnp.zeros(b.shape, F32)
     loads[1].wait()
     loads[0].wait()
 
@@ -184,13 +202,26 @@
             src_ref=src, dst_ref=dst, send_sem=ss, recv_sem=rs, device_id=dev, device_id_type=MESH
         )
 
-    pl.semaphore_wait(barrier, 6)
+    def start(copies):
+        for to, _, c in copies:
+            pl.when(to)(c.start)
+
+    def finish(copies):
+        for to, came, c in copies:
+            pl.when(came)(c.wait_recv)
+        for to, came, c in copies:
+            pl.when(to)(c.wait_send)
+
+    neighbours = (
+        jnp.where(has_left, 1, 0) + jnp.where(has_right, 1, 0) + jnp.where(has_above, 1, 0)
+        + jnp.where(has_below, 1, 0) + jnp.where(has_above2, 1, 0) + jnp.where(has_below2, 1, 0)
+    )
+    pl.semaphore_wait(barrier, neighbours)
     xcopies = [
-        remote(pk.at[0:2], from_left, xs_sem.at[0], xr_sem.at[0], (g, right)),
-        remote(pk.at[1:3], from_right, xs_sem.at[1], xr_sem.at[1], (g, left)),
+        (has_right, has_left, remote(pk.at[0:2], from_left, xs_sem.at[0], xr_sem.at[0], (g, right))),
+        (has_left, has_right, remote(pk.at[1:3], from_right, xs_sem.at[1], xr_sem.at[1], (g, left))),
     ]
-    for c in xcopies:
-        c.start()
+    start(xcopies)
 
     loads[3].wait()
     for l in range(LEVELS):
@@ -199,8 +230,7 @@
         for p in range(n):
             yo[OFF[l] + p] = r[:, p * BX : (p + 1) * BX]
 
-    for c in xcopies:
-        c.wait()
+    finish(xcopies)
     edge0 = dot(
         ayv[0], stacked(jnp.where(lane % 8 < 4, from_left[1], from_right[0]))
     )
@@ -233,14 +263,13 @@
                 send1[0, OFF[l] - NZ + p] = r[0:8]
                 send1[1, OFF[l] - NZ + p] = r[8:16]
     ycopies = [
-        remote(send0.at[0], recv0.at[0], ys_sem.at[0], yr_sem.at[0], (below, t)),
-        remote(send0.at[1], recv0.at[1], ys_sem.at[1], yr_sem.at[1], (above, t)),
-        remote(send1.at[0], recv1.at[0], ys_sem.at[2], yr_sem.at[2], (below, t)),
-        remote(send1.at[1], recv1.at[1], ys_sem.at[3], yr_sem.at[3], (above, t)),
-        remote(send1.at[0, 12:14], recv2, ys_sem.at[4], yr_sem.at[4], (below2, t)),
+        (has_below, has_above, remote(send0.at[0], recv0.at[0], ys_sem.at[0], yr_sem.at[0], (below, t))),
+        (has_above, has_below, remote(send0.at[1], recv0.at[1], ys_sem.at[1], yr_sem.at[1], (above, t))),
+        (has_below, has_above, remote(send1.at[0], recv1.at[0], ys_sem.at[2], yr_sem.at[2], (below, t))),
+        (has_above, has_below, remote(send1.at[1], recv1.at[1], ys_sem.at[3], yr_sem.at[3], (above, t))),
+        (has_below2, has_above2, remote(send1.at[0, 12:14], recv2, ys_sem.at[4], yr_sem.at[4], (below2, t))),
     ]
-    for c in ycopies:
-        c.start()
+    start(ycopies)
 
     row = lax.broadcasted_iota(jnp.int32, (BY, BX), 0)
     here = slice(0, BY)
@@ -258,8 +287,7 @@
                 value = jnp.where((row % step == 0) & (lane % step == 0), value, part)
         yo[z, :BY, :] = value
 
-    for c in ycopies:
-        c.wait()
+    finish(ycopies)
     lane = lanes_of((1, BX))
 
     def valid(l, p, j, v):

time: 25 us -> 17.5 us (0.70)
  the two profiles are of different devices: /device:TPU:2 before, /device:TPU:320 now
where the time goes in v2:
time: 17.5 us; the launch traced here: 17.4 us
  Pallas kernels  15.7 us (90%)
  local copies, waits for them, and re-layouts  1.62 us (9%)
    pallas_call x1, Pallas kernels, body(): pl.pallas_call(functools.partial(kernel, groups, tiles), out_shape=jax.Sh...  15.7 us
    unnamed x1, local copies, waits for them, and re-layouts  1.62 us

profile of v2, /device:TPU:320, one launch (start us, length us, event | category | flops | bytes accessed | tf_op | source)
XLA Modules:
  0.0 17.4 jit_solution(923060001551192345)
XLA Ops:
  0.0 15.7 %shard_map.46 = bf16[16,48,128]{2,1,0:T(8,128)(2,1)} custom-call(bf16[16,48,128]{2,1,0:T(8,128)(2,1)} %q_hbm.1, f32[1,16,48]{2,1,0:T(8,128)} %s_hbm.1, bf16[3,4,256,256]{3,2,1,0:T(8,128)(2,1)} %constant.4.clone.mx_hbm, bf16[8,4,64,144]{3,2,1,0:T(8,128)(2,1)} %constant.5.clone.ay_hbm), custom_call_target="tpu_custom_call" | custom-call | tf_op jit(solution)/shard_map/pallas_call | solution.py:327
  15.7 1.6 %copy.6 = bf16[16,48,128]{2,1,0:T(8,128)(2,1)} copy(bf16[16,48,128]{2,1,0:T(8,128)(2,1)} %shard_map.46) | data formatting | bytes 393216

commit v3 on v2

--- a/solution.py
+++ b/solution.py
@@ -121,7 +121,7 @@
     groups, tiles,
     q_hbm, s_hbm, mx_hbm, ay_hbm, out_ref,
     qv, sv, mxv, ayv, zh, zl, pk, from_left, from_right, yo,
-    send0, send1, recv0, recv1, recv2,
+    send0, send1, send2, recv0, recv1, recv2, recv3, recv4,
     load_sem, xs_sem, xr_sem, ys_sem, yr_sem,
 ):
     g, t = lax.axis_index("grp"), lax.axis_index("tile")
@@ -153,8 +153,9 @@
         c.start()
     for there, buffers in (
         (has_left, (from_left,)), (has_right, (from_right,)),
-        (has_above, (recv0.at[0], recv1.at[0])), (has_below, (recv0.at[1], recv1.at[1])),
-        (has_above2, (recv2,)),
+        (has_above, (recv0.at[0], recv1.at[0], recv3.at[0])),
+        (has_below, (recv0.at[1], recv1.at[1], recv3.at[1])),
+        (has_above2, (recv2, recv4)),
     ):
         @pl.when(jnp.logical_not(there))
         def _():
@@ -228,67 +229,78 @@
         n = NZ >> l
         r = dot(ayv[l], stacked(jnp.concatenate([own[l][p] for p in range(n)], axis=1)))
         for p in range(n):
-            yo[OFF[l] + p] = r[:, p * BX : (p + 1) * BX]
-
-    finish(xcopies)
-    edge0 = dot(
-        ayv[0], stacked(jnp.where(lane % 8 < 4, from_left[1], from_right[0]))
-    )
-    edges = dot(
-        ayv[1:].reshape(3 * (BY + 16), 3 * BY),
-        stacked(jnp.concatenate([from_left[0], from_right[1]], axis=1)),
-    )
-
-    def edge_of(l, p, rows):
-        n = rows.stop - rows.start
-        lane = lanes_of((n, BX))
-        win = 8 << l
-        turned = lambda e, s: pltpu.roll(e, (-s) % BX, 1)
-        if l == 0:
-            return jnp.where((lane + 4) % BX < 8, turned(edge0[rows], 8 * p), 0.0)
-        base = (l - 1) * (BY + 16)
-        e = edges[base + rows.start : base + rows.stop]
-        a = turned(e[:, :BX], win * p + SR[l])
-        b = turned(e[:, BX:], win * p + SL[l])
-        return jnp.where(lane < win, a, 0.0) + jnp.where(lane >= BX - win, b, 0.0)
-
-    tail = slice(BY, BY + 16)
-    for l in range(LEVELS):
-        for p in range(NZ >> l):
-            r = yo[OFF[l] + p, BY:, :] + edge_of(l, p, tail)
+            v = r[:, p * BX : (p + 1) * BX]
+            yo[OFF[l] + p] = v[:BY]
             if l == 0:
-                send0[0, p] = r[0:4]
-                send0[1, p] = r[12:16]
+                send0[0, p] = v[BY : BY + 4]
+                send0[1, p] = v[BY + 12 :]
             else:
-                send1[0, OFF[l] - NZ + p] = r[0:8]
-                send1[1, OFF[l] - NZ + p] = r[8:16]
-    ycopies = [
+                send1[0, OFF[l] - NZ + p] = v[BY : BY + 8]
+                send1[1, OFF[l] - NZ + p] = v[BY + 8 :]
+    y1copies = [
         (has_below, has_above, remote(send0.at[0], recv0.at[0], ys_sem.at[0], yr_sem.at[0], (below, t))),
         (has_above, has_below, remote(send0.at[1], recv0.at[1], ys_sem.at[1], yr_sem.at[1], (above, t))),
         (has_below, has_above, remote(send1.at[0], recv1.at[0], ys_sem.at[2], yr_sem.at[2], (below, t))),
         (has_above, has_below, remote(send1.at[1], recv1.at[1], ys_sem.at[3], yr_sem.at[3], (above, t))),
         (has_below2, has_above2, remote(send1.at[0, 12:14], recv2, ys_sem.at[4], yr_sem.at[4], (below2, t))),
     ]
-    start(ycopies)
+    start(y1copies)
+
+    finish(xcopies)
+    edge = stacked(
+        jnp.concatenate(
+            [jnp.where(lane % 8 < 4, from_left[1], from_right[0]), from_left[0], from_right[1]], axis=1
+        )
+    )
+    r = dot(jnp.concatenate([ayv[l, BY:] for l in range(LEVELS)], axis=0), edge)
+    far = [r[16 * l : 16 * l + 16] for l in range(LEVELS)]
+    part = lambda l, k: far[l][:, k * BX : (k + 1) * BX]
+    w = lanes_of((16, BX))
+    for k, v in enumerate((
+        part(0, 0),
+        jnp.where(w % 2 == 0, part(1, 1), jnp.where(w % 4 == 1, part(2, 1), part(3, 1))),
+        jnp.where(w % 2 == 1, part(1, 2), jnp.where(w % 4 == 2, part(2, 2), part(3, 2))),
+    )):
+        send2[0, k] = v[:8]
+        send2[1, k] = v[8:]
+    y2copies = [
+        (has_below, has_above, remote(send2.at[0], recv3.at[0], ys_sem.at[5], yr_sem.at[5], (below, t))),
+        (has_above, has_below, remote(send2.at[1], recv3.at[1], ys_sem.at[6], yr_sem.at[6], (above, t))),
+        (has_below2, has_above2, remote(send2.at[0], recv4, ys_sem.at[7], yr_sem.at[7], (below2, t))),
+    ]
+    start(y2copies)
+
+    def spread(l, p, packed0, packed_r, packed_l):
+        win = 8 << l
+        turned = lambda e, s: pltpu.roll(e, (-s) % BX, 1)
+        if l == 0:
+            return jnp.where((lanes_of(packed0.shape) + 4) % BX < 8, turned(packed0, 8 * p), 0.0)
+        w = lanes_of(packed_r.shape)
+        a = jnp.where(w < win, turned(packed_r, win * p + SR[l]), 0.0)
+        return a + jnp.where(w >= BX - win, turned(packed_l, win * p + SL[l]), 0.0)
+
+    r = dot(jnp.concatenate([ayv[l, :BY] for l in range(LEVELS)], axis=0), edge)
+    near = [r[BY * l : BY * l + BY] for l in range(LEVELS)]
 
     row = lax.broadcasted_iota(jnp.int32, (BY, BX), 0)
-    here = slice(0, BY)
     for z in range(NZ):
         value = None
         for l in reversed(range(LEVELS)):
             if z % (1 << l):
                 continue
             p = z >> l
-            part = yo[OFF[l] + p, :BY, :] + edge_of(l, p, here)
+            part = yo[OFF[l] + p] + spread(l, p, *(near[l][:, k * BX : (k + 1) * BX] for k in range(3)))
             if value is None:
                 value = part
             else:
                 step = 2 << l
                 value = jnp.where((row % step == 0) & (lane % step == 0), value, part)
-        yo[z, :BY, :] = value
-
-    finish(ycopies)
+        yo[z] = value
+
+    finish(y1copies)
+    finish(y2copies)
     lane = lanes_of((1, BX))
+    outer = [jnp.concatenate([recv3[0, k], recv3[1, k]], axis=0) for k in range(3)]
 
     def valid(l, p, j, v):
         if l and p % 2 == 0 and j % 2 == 0 and l < LEVELS - 1:
@@ -305,19 +317,22 @@
             if z % (1 << l):
                 continue
             p = z >> l
+            e = spread(l, p, *outer)
+            if l == 0:
+                down, up = recv0[0, p] + e[:4], recv0[1, p] + e[12:]
+            else:
+                down, up = recv1[0, OFF[l] - NZ + p] + e[:8], recv1[1, OFF[l] - NZ + p] + e[8:]
             for k in range(3 if l == 0 else 7):
                 if k << l < BY:
-                    v = recv0[0, p, k : k + 1, :] if l == 0 else recv1[0, OFF[l] - NZ + p, k : k + 1, :]
-                    adds.setdefault(k << l, []).append(valid(l, p, k, v))
+                    adds.setdefault(k << l, []).append(valid(l, p, k, down[k : k + 1]))
             for k in range(4 if l == 0 else 2, 8):
-                r = BY - ((8 - k) << l)
-                v = recv0[1, p, k - 4 : k - 3, :] if l == 0 else recv1[1, OFF[l] - NZ + p, k : k + 1, :]
-                adds.setdefault(r, []).append(valid(l, p, k, v))
+                adds.setdefault(BY - ((8 - k) << l), []).append(valid(l, p, k, up[k - 4 : k - 3] if l == 0 else up[k : k + 1]))
             if l == 3:
-                adds[0].append(valid(l, p, 6, recv2[p, 6:7, :]))
+                v = recv2[p] + spread(l, p, None, recv4[1], recv4[2])
+                adds[0].append(valid(l, p, 6, v[6:7]))
         for r, vs in adds.items():
             yo[z, r : r + 1, :] = functools.reduce(lambda a, b: a + b, vs, yo[z, r : r + 1, :])
-        out_ref[z] = yo[z, :BY, :].astype(BF16)
+        out_ref[z] = yo[z].astype(BF16)
 
 
 def body(quantized, scales):
@@ -326,9 +341,9 @@
     dma = pltpu.SemaphoreType.DMA
     return pl.pallas_call(
         functools.partial(kernel, groups, tiles),
-        out_shape=jax.ShapeDtypeStruct((NZ, BY, BX), BF16),
+        out_shape=pltpu.VMEM((NZ, BY, BX), BF16),
         in_specs=[hbm] * 4,
-        out_specs=pl.BlockSpec(memory_space=pltpu.VMEM),
+
         scratch_shapes=[
             pltpu.VMEM((NZ, BY, BX), BF16),
             pltpu.VMEM((1, NZ, BY), F32),
@@ -339,13 +354,16 @@
             pltpu.VMEM((3, BY, BX), F32),
             pltpu.VMEM((2, BY, BX), F32),
             pltpu.VMEM((2, BY, BX), F32),
-            pltpu.VMEM((NP, BY + 16, BX), F32),
+            pltpu.VMEM((NP, BY, BX), F32),
             pltpu.VMEM((2, NZ, 4, BX), F32),
             pltpu.VMEM((2, NP - NZ, 8, BX), F32),
+            pltpu.VMEM((2, 3, 8, BX), F32),
             pltpu.VMEM((2, NZ, 4, BX), F32),
             pltpu.VMEM((2, NP - NZ, 8, BX), F32),
             pltpu.VMEM((2, 8, BX), F32),
-            dma((4,)), dma((2,)), dma((2,)), dma((5,)), dma((5,)),
+            pltpu.VMEM((2, 3, 8, BX), F32),
+            pltpu.VMEM((3, 8, BX), F32),
+            dma((4,)), dma((2,)), dma((2,)), dma((8,)), dma((8,)),
         ],
         compiler_params=pltpu.CompilerParams(collective_id=0, has_side_effects=True),
     )(quantized, scales, jnp.asarray(x_matrices()), jnp.asarray(y_matrices(groups)))

time: 17.5 us -> 15.1 us (0.86)
  Pallas kernels: 15.7 us -> 14.3 us
  local copies, waits for them, and re-layouts: 1.62 us -> 0.68 us
    pallas_call x1, Pallas kernels: 15.7 us -> 14.3 us  [body(): pl.pallas_call(functools.partial(kernel, groups, tiles), out_shape=pltpu....]
    unnamed x1, local copies, waits for them, and re-layouts: 1.62 us -> 0.68 us
where the time goes in v3:
time: 15.1 us; the launch traced here: 15 us
  Pallas kernels  14.3 us (95%)
  local copies, waits for them, and re-layouts  0.68 us (5%)
    pallas_call x1, Pallas kernels, body(): pl.pallas_call(functools.partial(kernel, groups, tiles), out_shape=pltpu....  14.3 us
    unnamed x1, local copies, waits for them, and re-layouts  0.68 us

profile of v3, /device:TPU:320, one launch (start us, length us, event | category | flops | bytes accessed | tf_op | source)
XLA Modules:
  0.0 15.0 jit_solution(5679470168563229224)
XLA Ops:
  0.0 14.3 %shard_map.46 = bf16[16,48,128]{2,1,0:T(8,128)(2,1)S(1)} custom-call(bf16[16,48,128]{2,1,0:T(8,128)(2,1)} %q_hbm.1, f32[1,16,48]{2,1,0:T(8,128)} %s_hbm.1, bf16[3,4,256,256]{3,2,1,0:T(8,128)(2,1)} %constant.4.clone.mx_hbm, bf16[8,4,64,144]{3,2,1,0:T(8,128)(2,1)} %constant.5.clone.ay_hbm), custom_call_target="tpu_custom_call" | custom-call | tf_op jit(solution)/shard_map/pallas_call | solution.py:342
  14.3 0.7 %copy.6 = bf16[16,48,128]{2,1,0:T(8,128)(2,1)} copy(bf16[16,48,128]{2,1,0:T(8,128)(2,1)S(1)} %shard_map.46) | data formatting | bytes 393216

commit v4 on v3

--- a/solution.py
+++ b/solution.py
@@ -20,6 +20,7 @@
 NP = 30
 SR = (0, 0, 1, 3)
 SL = (0, 1, 2, 0)
+SLOT = (0, 0, 4, 5)
 MESH = pl.DeviceIdType.MESH
 F32, BF16 = jnp.float32, jnp.bfloat16
 
@@ -51,6 +52,11 @@
     hi = a.astype(np.float32).astype(BF16)
     lo = (a - hi.astype(np.float64)).astype(np.float32).astype(BF16)
     return hi, lo
+
+
+def hi_hi_lo(a):
+    hi, lo = split(a)
+    return np.concatenate([hi, hi, lo], axis=-1)
 
 
 @functools.cache
@@ -95,8 +101,17 @@
                 r = g * b - 8 + k
                 if r >= max((g - 1) * b, 0):
                     m[g, l, BY + 8 + k] = mine[r]
-    hi, lo = split(m)
-    return np.concatenate([hi, hi, lo], axis=3)
+    return hi_hi_lo(m)
+
+
+@functools.cache
+def packed_matrices(groups):
+    m = y_matrices(groups)
+    out = np.zeros((groups, LEVELS - 1, 40, 3 * BY), m.dtype)
+    for l in range(1, LEVELS):
+        out[:, l - 1, : BY >> l] = m[:, l, : BY : 1 << l]
+        out[:, l - 1, 24:] = m[:, l, BY:]
+    return out
 
 
 def hilo(x):
@@ -119,8 +134,8 @@
 
 def kernel(
     groups, tiles,
-    q_hbm, s_hbm, mx_hbm, ay_hbm, out_ref,
-    qv, sv, mxv, ayv, zh, zl, pk, from_left, from_right, yo,
+    q_hbm, s_hbm, mx_hbm, ay_hbm, ac_hbm, out_ref,
+    qv, sv, mxv, ayv, acv, zh, zl, to_right, to_left, from_left, from_right, wide, yo,
     send0, send1, send2, recv0, recv1, recv2, recv3, recv4,
     load_sem, xs_sem, xr_sem, ys_sem, yr_sem,
 ):
@@ -148,6 +163,7 @@
         pltpu.make_async_copy(s_hbm, sv, load_sem.at[1]),
         pltpu.make_async_copy(mx_hbm.at[side], mxv, load_sem.at[2]),
         pltpu.make_async_copy(ay_hbm.at[g], ayv, load_sem.at[3]),
+        pltpu.make_async_copy(ac_hbm.at[g], acv, load_sem.at[4]),
     ]
     for c in loads:
         c.start()
@@ -189,14 +205,24 @@
         if l == 0:
             plane = ((lane + 4) // 8) % NZ
         else:
-            to_right = (lane % (1 << l)) == SR[l] % (1 << l)
-            plane = jnp.where(to_right, lane // win, (lane // win + 1) % n)
+            rightward = (lane % (1 << l)) == SR[l] % (1 << l)
+            plane = jnp.where(rightward, lane // win, (lane // win + 1) % n)
         which = lax.broadcasted_iota(jnp.int32, (n, 1, BX), 0)
         packs.append(jnp.sum(jnp.where(which == plane, r[:, BX:].reshape(n, BY, BX), 0.0), axis=0))
+
+    loads[3].wait()
+    loads[4].wait()
+    e0 = dot(ayv[0], stacked(packs[0]))
+    e1, e2, e3 = (dot(acv[l - 1], stacked(packs[l])) for l in range(1, LEVELS))
+    lane = lanes_of((24, BX))
+    to_right[:24] = jnp.where(lane % 8 < 4, e0[:24], pltpu.roll(e0[24:48], 4, 1))
+    to_left[:24] = jnp.where(lane % 8 >= 4, e0[:24], pltpu.roll(e0[24:48], BX - 4, 1))
+    to_right[24:32] = e0[48:56] + e0[56:]
+    to_left[24:32] = e0[48:56] + e0[56:]
+    lane = lanes_of((40, BX))
+    to_right[32:] = jnp.where(lane % 2 == 0, e1, jnp.where(lane % 4 == 1, e2, e3))
+    to_left[32:] = jnp.where(lane % 2 == 1, e1, jnp.where(lane % 4 == 2, e2, e3))
     lane = lanes_of((BY, BX))
-    pk[0] = jnp.where(lane % 2 == 0, packs[1], jnp.where(lane % 4 == 1, packs[2], packs[3]))
-    pk[1] = packs[0]
-    pk[2] = jnp.where(lane % 2 == 1, packs[1], jnp.where(lane % 4 == 2, packs[2], packs[3]))
 
     def remote(src, dst, ss, rs, dev):
         return pltpu.make_async_remote_copy(
@@ -219,50 +245,42 @@
     )
     pl.semaphore_wait(barrier, neighbours)
     xcopies = [
-        (has_right, has_left, remote(pk.at[0:2], from_left, xs_sem.at[0], xr_sem.at[0], (g, right))),
-        (has_left, has_right, remote(pk.at[1:3], from_right, xs_sem.at[1], xr_sem.at[1], (g, left))),
+        (has_right, has_left, remote(to_right, from_left, xs_sem.at[0], xr_sem.at[0], (g, right))),
+        (has_left, has_right, remote(to_left, from_right, xs_sem.at[1], xr_sem.at[1], (g, left))),
     ]
     start(xcopies)
 
-    loads[3].wait()
     for l in range(LEVELS):
         n = NZ >> l
         r = dot(ayv[l], stacked(jnp.concatenate([own[l][p] for p in range(n)], axis=1)))
+        tail = [r[BY:, p * BX : (p + 1) * BX] for p in range(n)]
         for p in range(n):
-            v = r[:, p * BX : (p + 1) * BX]
-            yo[OFF[l] + p] = v[:BY]
+            yo[OFF[l] + p] = r[:BY, p * BX : (p + 1) * BX]
             if l == 0:
-                send0[0, p] = v[BY : BY + 4]
-                send0[1, p] = v[BY + 12 :]
-            else:
-                send1[0, OFF[l] - NZ + p] = v[BY : BY + 8]
-                send1[1, OFF[l] - NZ + p] = v[BY + 8 :]
+                send0[0, p] = tail[p][:4]
+                send0[1, p] = tail[p][12:]
+        for first in range(0, n, 1 << l) if l else ():
+            both = tail[first]
+            for p in range(first + 1, min(first + (1 << l), n)):
+                both = both + pltpu.roll(tail[p], p - first, 1)
+            send1[0, SLOT[l] + (first >> l)] = both[:8]
+            send1[1, SLOT[l] + (first >> l)] = both[8:]
     y1copies = [
         (has_below, has_above, remote(send0.at[0], recv0.at[0], ys_sem.at[0], yr_sem.at[0], (below, t))),
         (has_above, has_below, remote(send0.at[1], recv0.at[1], ys_sem.at[1], yr_sem.at[1], (above, t))),
         (has_below, has_above, remote(send1.at[0], recv1.at[0], ys_sem.at[2], yr_sem.at[2], (below, t))),
         (has_above, has_below, remote(send1.at[1], recv1.at[1], ys_sem.at[3], yr_sem.at[3], (above, t))),
-        (has_below2, has_above2, remote(send1.at[0, 12:14], recv2, ys_sem.at[4], yr_sem.at[4], (below2, t))),
+        (has_below2, has_above2, remote(send1.at[0, SLOT[3]], recv2, ys_sem.at[4], yr_sem.at[4], (below2, t))),
     ]
     start(y1copies)
 
     finish(xcopies)
-    edge = stacked(
-        jnp.concatenate(
-            [jnp.where(lane % 8 < 4, from_left[1], from_right[0]), from_left[0], from_right[1]], axis=1
-        )
-    )
-    r = dot(jnp.concatenate([ayv[l, BY:] for l in range(LEVELS)], axis=0), edge)
-    far = [r[16 * l : 16 * l + 16] for l in range(LEVELS)]
-    part = lambda l, k: far[l][:, k * BX : (k + 1) * BX]
-    w = lanes_of((16, BX))
-    for k, v in enumerate((
-        part(0, 0),
-        jnp.where(w % 2 == 0, part(1, 1), jnp.where(w % 4 == 1, part(2, 1), part(3, 1))),
-        jnp.where(w % 2 == 1, part(1, 2), jnp.where(w % 4 == 2, part(2, 2), part(3, 2))),
-    )):
-        send2[0, k] = v[:8]
-        send2[1, k] = v[8:]
+    w = lanes_of((8, BX))
+    middle = jnp.where(w % 8 < 4, from_left[24:32], from_right[24:32])
+    for k in range(2):
+        send2[k, 0] = middle
+        send2[k, 1] = from_left[56 + 8 * k : 64 + 8 * k]
+        send2[k, 2] = from_right[56 + 8 * k : 64 + 8 * k]
     y2copies = [
         (has_below, has_above, remote(send2.at[0], recv3.at[0], ys_sem.at[5], yr_sem.at[5], (below, t))),
         (has_above, has_below, remote(send2.at[1], recv3.at[1], ys_sem.at[6], yr_sem.at[6], (above, t))),
@@ -279,8 +297,14 @@
         a = jnp.where(w < win, turned(packed_r, win * p + SR[l]), 0.0)
         return a + jnp.where(w >= BX - win, turned(packed_l, win * p + SL[l]), 0.0)
 
-    r = dot(jnp.concatenate([ayv[l, :BY] for l in range(LEVELS)], axis=0), edge)
-    near = [r[BY * l : BY * l + BY] for l in range(LEVELS)]
+    a, b = from_left[:24], from_right[:24]
+    w = lanes_of((24, BX)) % 8 < 4
+    wide[0, 0, :24] = jnp.where(w, a, b)
+    wide[0, 0, 24:] = jnp.where(w, pltpu.roll(a, BX - 4, 1), pltpu.roll(b, 4, 1))
+    for l in range(1, LEVELS):
+        n = BY >> l
+        wide[l, 0, pl.ds(0, n, stride=1 << l), :] = from_left[32 : 32 + n]
+        wide[l, 1, pl.ds(0, n, stride=1 << l), :] = from_right[32 : 32 + n]
 
     row = lax.broadcasted_iota(jnp.int32, (BY, BX), 0)
     for z in range(NZ):
@@ -289,7 +313,7 @@
             if z % (1 << l):
                 continue
             p = z >> l
-            part = yo[OFF[l] + p] + spread(l, p, *(near[l][:, k * BX : (k + 1) * BX] for k in range(3)))
+            part = yo[OFF[l] + p] + spread(l, p, wide[l, 0], wide[l, 0], wide[l, 1])
             if value is None:
                 value = part
             else:
@@ -321,14 +345,16 @@
             if l == 0:
                 down, up = recv0[0, p] + e[:4], recv0[1, p] + e[12:]
             else:
-                down, up = recv1[0, OFF[l] - NZ + p] + e[:8], recv1[1, OFF[l] - NZ + p] + e[8:]
+                slot, turn = SLOT[l] + (p >> l), (BX - p % (1 << l)) % BX
+                down = pltpu.roll(recv1[0, slot], turn, 1) + e[:8]
+                up = pltpu.roll(recv1[1, slot], turn, 1) + e[8:]
             for k in range(3 if l == 0 else 7):
                 if k << l < BY:
                     adds.setdefault(k << l, []).append(valid(l, p, k, down[k : k + 1]))
             for k in range(4 if l == 0 else 2, 8):
                 adds.setdefault(BY - ((8 - k) << l), []).append(valid(l, p, k, up[k - 4 : k - 3] if l == 0 else up[k : k + 1]))
             if l == 3:
-                v = recv2[p] + spread(l, p, None, recv4[1], recv4[2])
+                v = pltpu.roll(recv2[...], turn, 1) + spread(l, p, None, recv4[1], recv4[2])
                 adds[0].append(valid(l, p, 6, v[6:7]))
         for r, vs in adds.items():
             yo[z, r : r + 1, :] = functools.reduce(lambda a, b: a + b, vs, yo[z, r : r + 1, :])
@@ -342,31 +368,35 @@
     return pl.pallas_call(
         functools.partial(kernel, groups, tiles),
         out_shape=pltpu.VMEM((NZ, BY, BX), BF16),
-        in_specs=[hbm] * 4,
+        in_specs=[hbm] * 5,
 
         scratch_shapes=[
             pltpu.VMEM((NZ, BY, BX), BF16),
             pltpu.VMEM((1, NZ, BY), F32),
             pltpu.VMEM((LEVELS, 2 * BX, 2 * BX), BF16),
             pltpu.VMEM((LEVELS, BY + 16, 3 * BY), BF16),
+            pltpu.VMEM((LEVELS - 1, 40, 3 * BY), BF16),
             pltpu.VMEM((NP, BY, BX), BF16),
             pltpu.VMEM((NP, BY, BX), BF16),
-            pltpu.VMEM((3, BY, BX), F32),
-            pltpu.VMEM((2, BY, BX), F32),
-            pltpu.VMEM((2, BY, BX), F32),
+            pltpu.VMEM((72, BX), F32),
+            pltpu.VMEM((72, BX), F32),
+            pltpu.VMEM((72, BX), F32),
+            pltpu.VMEM((72, BX), F32),
+            pltpu.VMEM((LEVELS, 2, BY, BX), F32),
             pltpu.VMEM((NP, BY, BX), F32),
             pltpu.VMEM((2, NZ, 4, BX), F32),
-            pltpu.VMEM((2, NP - NZ, 8, BX), F32),
+            pltpu.VMEM((2, 6, 8, BX), F32),
             pltpu.VMEM((2, 3, 8, BX), F32),
             pltpu.VMEM((2, NZ, 4, BX), F32),
-            pltpu.VMEM((2, NP - NZ, 8, BX), F32),
-            pltpu.VMEM((2, 8, BX), F32),
+            pltpu.VMEM((2, 6, 8, BX), F32),
+            pltpu.VMEM((8, BX), F32),
             pltpu.VMEM((2, 3, 8, BX), F32),
             pltpu.VMEM((3, 8, BX), F32),
-            dma((4,)), dma((2,)), dma((2,)), dma((8,)), dma((8,)),
+            dma((5,)), dma((2,)), dma((2,)), dma((8,)), dma((8,)),
         ],
         compiler_params=pltpu.CompilerParams(collective_id=0, has_side_effects=True),
-    )(quantized, scales, jnp.asarray(x_matrices()), jnp.asarray(y_matrices(groups)))
+    )(quantized, scales, jnp.asarray(x_matrices()), jnp.asarray(y_matrices(groups)),
+      jnp.asarray(packed_matrices(groups)))
 
 
 def solution(mesh):

time: 15.1 us -> 14.7 us (0.974)
  Pallas kernels: 14.3 us -> 13.9 us
    pallas_call x1, Pallas kernels: 14.3 us -> 13.9 us  [body(): pl.pallas_call(functools.partial(kernel, groups, tiles), out_shape=pltpu....]
where the time goes in v4:
time: 14.7 us; the launch traced here: 14.6 us
  Pallas kernels  13.9 us (95%)
  local copies, waits for them, and re-layouts  0.68 us (5%)
    pallas_call x1, Pallas kernels, body(): pl.pallas_call(functools.partial(kernel, groups, tiles), out_shape=pltpu....  13.9 us
    unnamed x1, local copies, waits for them, and re-layouts  0.68 us

profile of v4, /device:TPU:320, one launch (start us, length us, event | category | flops | bytes accessed | tf_op | source)
XLA Modules:
  0.0 14.6 jit_solution(6218673063645587527)
XLA Ops:
  0.0 13.9 %shard_map.55 = bf16[16,48,128]{2,1,0:T(8,128)(2,1)S(1)} custom-call(bf16[16,48,128]{2,1,0:T(8,128)(2,1)} %q_hbm.1, f32[1,16,48]{2,1,0:T(8,128)} %s_hbm.1, bf16[3,4,256,256]{3,2,1,0:T(8,128)(2,1)} %constant.6.clone.mx_hbm, bf16[8,4,64,144]{3,2,1,0:T(8,128)(2,1)} %constant.7.clone.ay_hbm, bf16[8,3,40,144]{3,2,1,0:T(8,128)(2,1)} %constant.8.clone.ac_hbm), custom_call_target="tpu_custom_call" | custom-call | tf_op jit(solution)/shard_map/pallas_call | solution.py:368
  13.9 0.7 %copy.7 = bf16[16,48,128]{2,1,0:T(8,128)(2,1)} copy(bf16[16,48,128]{2,1,0:T(8,128)(2,1)S(1)} %shard_map.55) | data formatting | bytes 393216

commit v5 on v4

--- a/solution.py
+++ b/solution.py
@@ -135,8 +135,9 @@
 def kernel(
     groups, tiles,
     q_hbm, s_hbm, mx_hbm, ay_hbm, ac_hbm, out_ref,
-    qv, sv, mxv, ayv, acv, zh, zl, to_right, to_left, from_left, from_right, wide, yo,
-    send0, send1, send2, recv0, recv1, recv2, recv3, recv4,
+    qv, sv, mxv, ayv, acv, zh, zl, to_right, to_left, from_left, from_right,
+    to_right_far, to_left_far, from_left_far, from_right_far, wide, wide2, yo,
+    send0, send1, recv0, recv1, recv2, down2, up2, down3,
     load_sem, xs_sem, xr_sem, ys_sem, yr_sem,
 ):
     g, t = lax.axis_index("grp"), lax.axis_index("tile")
@@ -168,10 +169,11 @@
     for c in loads:
         c.start()
     for there, buffers in (
-        (has_left, (from_left,)), (has_right, (from_right,)),
-        (has_above, (recv0.at[0], recv1.at[0], recv3.at[0])),
-        (has_below, (recv0.at[1], recv1.at[1], recv3.at[1])),
-        (has_above2, (recv2, recv4)),
+        (has_left, (from_left, from_left_far)),
+        (has_right, (from_right, from_right_far)),
+        (has_above, (recv0.at[0], recv1.at[0], down2)),
+        (has_below, (recv0.at[1], recv1.at[1], up2)),
+        (has_above2, (recv2, down3)),
     ):
         @pl.when(jnp.logical_not(there))
         def _():
@@ -214,14 +216,18 @@
     loads[4].wait()
     e0 = dot(ayv[0], stacked(packs[0]))
     e1, e2, e3 = (dot(acv[l - 1], stacked(packs[l])) for l in range(1, LEVELS))
+    lane = lanes_of((40, BX))
+    rightward = jnp.where(lane % 2 == 0, e1, jnp.where(lane % 4 == 1, e2, e3))
+    leftward = jnp.where(lane % 2 == 1, e1, jnp.where(lane % 4 == 2, e2, e3))
+    for far, v in ((to_right_far, rightward), (to_left_far, leftward)):
+        far[:8] = v[24:32]
+        far[8:16] = e0[48:56] + e0[56:]
+        far[16:] = v[32:]
     lane = lanes_of((24, BX))
     to_right[:24] = jnp.where(lane % 8 < 4, e0[:24], pltpu.roll(e0[24:48], 4, 1))
     to_left[:24] = jnp.where(lane % 8 >= 4, e0[:24], pltpu.roll(e0[24:48], BX - 4, 1))
-    to_right[24:32] = e0[48:56] + e0[56:]
-    to_left[24:32] = e0[48:56] + e0[56:]
-    lane = lanes_of((40, BX))
-    to_right[32:] = jnp.where(lane % 2 == 0, e1, jnp.where(lane % 4 == 1, e2, e3))
-    to_left[32:] = jnp.where(lane % 2 == 1, e1, jnp.where(lane % 4 == 2, e2, e3))
+    to_right[24:] = rightward[:24]
+    to_left[24:] = leftward[:24]
     lane = lanes_of((BY, BX))
 
     def remote(src, dst, ss, rs, dev):
@@ -244,9 +250,14 @@
         + jnp.where(has_below, 1, 0) + jnp.where(has_above2, 1, 0) + jnp.where(has_below2, 1, 0)
     )
     pl.semaphore_wait(barrier, neighbours)
+    farcopies = [
+        (has_right, has_left, remote(to_right_far, from_left_far, xs_sem.at[0], xr_sem.at[0], (g, right))),
+        (has_left, has_right, remote(to_left_far, from_right_far, xs_sem.at[1], xr_sem.at[1], (g, left))),
+    ]
+    start(farcopies)
     xcopies = [
-        (has_right, has_left, remote(to_right, from_left, xs_sem.at[0], xr_sem.at[0], (g, right))),
-        (has_left, has_right, remote(to_left, from_right, xs_sem.at[1], xr_sem.at[1], (g, left))),
+        (has_right, has_left, remote(to_right, from_left, xs_sem.at[2], xr_sem.at[2], (g, right))),
+        (has_left, has_right, remote(to_left, from_right, xs_sem.at[3], xr_sem.at[3], (g, left))),
     ]
     start(xcopies)
 
@@ -274,37 +285,35 @@
     ]
     start(y1copies)
 
-    finish(xcopies)
-    w = lanes_of((8, BX))
-    middle = jnp.where(w % 8 < 4, from_left[24:32], from_right[24:32])
-    for k in range(2):
-        send2[k, 0] = middle
-        send2[k, 1] = from_left[56 + 8 * k : 64 + 8 * k]
-        send2[k, 2] = from_right[56 + 8 * k : 64 + 8 * k]
-    y2copies = [
-        (has_below, has_above, remote(send2.at[0], recv3.at[0], ys_sem.at[5], yr_sem.at[5], (below, t))),
-        (has_above, has_below, remote(send2.at[1], recv3.at[1], ys_sem.at[6], yr_sem.at[6], (above, t))),
-        (has_below2, has_above2, remote(send2.at[0], recv4, ys_sem.at[7], yr_sem.at[7], (below2, t))),
-    ]
+    finish(farcopies)
+    y2copies = []
+    for k, far in enumerate((from_left_far, from_right_far)):
+        y2copies += [
+            (has_below, has_above, remote(far.at[:16], down2.at[k], ys_sem.at[5 + k], yr_sem.at[5 + k], (below, t))),
+            (has_above, has_below, remote(far.at[8:], up2.at[k], ys_sem.at[7 + k], yr_sem.at[7 + k], (above, t))),
+            (has_below2, has_above2, remote(far.at[:8], down3.at[k], ys_sem.at[9 + k], yr_sem.at[9 + k], (below2, t))),
+        ]
     start(y2copies)
 
-    def spread(l, p, packed0, packed_r, packed_l):
+    def spread(l, p, packed0, packed_r, packed_l, keep=None):
         win = 8 << l
         turned = lambda e, s: pltpu.roll(e, (-s) % BX, 1)
+        both = (lambda m: m) if keep is None else (lambda m: jnp.logical_and(m, keep))
         if l == 0:
-            return jnp.where((lanes_of(packed0.shape) + 4) % BX < 8, turned(packed0, 8 * p), 0.0)
+            return jnp.where(both((lanes_of(packed0.shape) + 4) % BX < 8), turned(packed0, 8 * p), 0.0)
         w = lanes_of(packed_r.shape)
-        a = jnp.where(w < win, turned(packed_r, win * p + SR[l]), 0.0)
-        return a + jnp.where(w >= BX - win, turned(packed_l, win * p + SL[l]), 0.0)
-
+        a = jnp.where(both(w < win), turned(packed_r, win * p + SR[l]), 0.0)
+        return a + jnp.where(both(w >= BX - win), turned(packed_l, win * p + SL[l]), 0.0)
+
+    finish(xcopies)
     a, b = from_left[:24], from_right[:24]
     w = lanes_of((24, BX)) % 8 < 4
     wide[0, 0, :24] = jnp.where(w, a, b)
     wide[0, 0, 24:] = jnp.where(w, pltpu.roll(a, BX - 4, 1), pltpu.roll(b, 4, 1))
     for l in range(1, LEVELS):
         n = BY >> l
-        wide[l, 0, pl.ds(0, n, stride=1 << l), :] = from_left[32 : 32 + n]
-        wide[l, 1, pl.ds(0, n, stride=1 << l), :] = from_right[32 : 32 + n]
+        wide[l, 0, pl.ds(0, n, stride=1 << l), :] = from_left[24 : 24 + n]
+        wide[l, 1, pl.ds(0, n, stride=1 << l), :] = from_right[24 : 24 + n]
 
     row = lax.broadcasted_iota(jnp.int32, (BY, BX), 0)
     for z in range(NZ):
@@ -321,10 +330,9 @@
                 value = jnp.where((row % step == 0) & (lane % step == 0), value, part)
         yo[z] = value
 
+    wide2[...] = jnp.zeros(wide2.shape, F32)
     finish(y1copies)
-    finish(y2copies)
     lane = lanes_of((1, BX))
-    outer = [jnp.concatenate([recv3[0, k], recv3[1, k]], axis=0) for k in range(3)]
 
     def valid(l, p, j, v):
         if l and p % 2 == 0 and j % 2 == 0 and l < LEVELS - 1:
@@ -341,24 +349,52 @@
             if z % (1 << l):
                 continue
             p = z >> l
-            e = spread(l, p, *outer)
             if l == 0:
-                down, up = recv0[0, p] + e[:4], recv0[1, p] + e[12:]
+                down, up = recv0[0, p], recv0[1, p]
             else:
                 slot, turn = SLOT[l] + (p >> l), (BX - p % (1 << l)) % BX
-                down = pltpu.roll(recv1[0, slot], turn, 1) + e[:8]
-                up = pltpu.roll(recv1[1, slot], turn, 1) + e[8:]
+                down = pltpu.roll(recv1[0, slot], turn, 1)
+                up = pltpu.roll(recv1[1, slot], turn, 1)
             for k in range(3 if l == 0 else 7):
                 if k << l < BY:
                     adds.setdefault(k << l, []).append(valid(l, p, k, down[k : k + 1]))
             for k in range(4 if l == 0 else 2, 8):
                 adds.setdefault(BY - ((8 - k) << l), []).append(valid(l, p, k, up[k - 4 : k - 3] if l == 0 else up[k : k + 1]))
             if l == 3:
-                v = pltpu.roll(recv2[...], turn, 1) + spread(l, p, None, recv4[1], recv4[2])
+                v = pltpu.roll(recv2[...], turn, 1)
                 adds[0].append(valid(l, p, 6, v[6:7]))
         for r, vs in adds.items():
             yo[z, r : r + 1, :] = functools.reduce(lambda a, b: a + b, vs, yo[z, r : r + 1, :])
-        out_ref[z] = yo[z].astype(BF16)
+
+    finish(y2copies)
+    for k in range(2):
+        for l in range(1, LEVELS):
+            n, rows = min(7, BY >> l), wide2.at[l - 1, k]
+            rows[pl.ds(0, n, stride=1 << l), :] = down2[k, :n]
+            last = pl.ds(BY - (6 << l), 6, stride=1 << l)
+            rows[last, :] = rows[last, :] + up2[k, 10:]
+        wide2[2, k, 0:1] = wide2[2, k, 0:1] + down3[k, 6:7]
+    w, r = lanes_of((8, BX)), lax.broadcasted_iota(jnp.int32, (8, BX), 0)
+    top = jnp.where(w % 8 < 4, down2[0, 8:], down2[1, 8:])
+    low = jnp.where(w % 8 < 4, up2[0, :8], up2[1, :8])
+    ends = jnp.where(r < 4, top, low)
+    not_lower = jnp.logical_or(r % 2 == 1, w % 2 == 1)
+    for z in range(NZ):
+        tiles = [yo[z, 8 * i : 8 * i + 8, :] for i in range(6)]
+        e = spread(0, z, ends, None, None, not_lower if z % 2 == 0 else None)
+        tiles[0] = tiles[0] + jnp.where(r < 4, e, 0.0)
+        tiles[5] = tiles[5] + jnp.where(r < 4, 0.0, e)
+        for l in range(1, LEVELS):
+            if z % (1 << l):
+                continue
+            p = z >> l
+            for i in (0, 1, 4, 5) if l == 1 else range(6):
+                keep = w % (1 << l) == 0
+                if p % 2 == 0 and l < LEVELS - 1:
+                    keep = jnp.logical_and(keep, jnp.logical_or(r % (2 << l) > 0, w % (2 << l) > 0))
+                a, b = (wide2[l - 1, k, 8 * i : 8 * i + 8, :] for k in range(2))
+                tiles[i] = tiles[i] + spread(l, p, None, a, b, keep)
+        out_ref[z] = jnp.concatenate(tiles, axis=0).astype(BF16)
 
 
 def body(quantized, scales):
@@ -378,21 +414,20 @@
             pltpu.VMEM((LEVELS - 1, 40, 3 * BY), BF16),
             pltpu.VMEM((NP, BY, BX), BF16),
             pltpu.VMEM((NP, BY, BX), BF16),
-            pltpu.VMEM((72, BX), F32),
-            pltpu.VMEM((72, BX), F32),
-            pltpu.VMEM((72, BX), F32),
-            pltpu.VMEM((72, BX), F32),
+            *[pltpu.VMEM((BY, BX), F32) for _ in range(4)],
+            *[pltpu.VMEM((24, BX), F32) for _ in range(4)],
             pltpu.VMEM((LEVELS, 2, BY, BX), F32),
+            pltpu.VMEM((LEVELS - 1, 2, BY, BX), F32),
             pltpu.VMEM((NP, BY, BX), F32),
             pltpu.VMEM((2, NZ, 4, BX), F32),
             pltpu.VMEM((2, 6, 8, BX), F32),
-            pltpu.VMEM((2, 3, 8, BX), F32),
             pltpu.VMEM((2, NZ, 4, BX), F32),
             pltpu.VMEM((2, 6, 8, BX), F32),
             pltpu.VMEM((8, BX), F32),
-            pltpu.VMEM((2, 3, 8, BX), F32),
-            pltpu.VMEM((3, 8, BX), F32),
-            dma((5,)), dma((2,)), dma((2,)), dma((8,)), dma((8,)),
+            pltpu.VMEM((2, 16, BX), F32),
+            pltpu.VMEM((2, 16, BX), F32),
+            pltpu.VMEM((2, 8, BX), F32),
+            dma((5,)), dma((4,)), dma((4,)), dma((11,)), dma((11,)),
         ],
         compiler_params=pltpu.CompilerParams(collective_id=0, has_side_effects=True),
     )(quantized, scales, jnp.asarray(x_matrices()), jnp.asarray(y_matrices(groups)),

time: 14.7 us -> 14.2 us (0.966)
  Pallas kernels: 13.9 us -> 13.4 us
    pallas_call x1, Pallas kernels: 13.9 us -> 13.4 us  [body(): pl.pallas_call(functools.partial(kernel, groups, tiles), out_shape=pltpu....]
where the time goes in v5:
time: 14.2 us; the launch traced here: 14.1 us
  Pallas kernels  13.4 us (94%)
  local copies, waits for them, and re-layouts  0.68 us (5%)
    pallas_call x1, Pallas kernels, body(): pl.pallas_call(functools.partial(kernel, groups, tiles), out_shape=pltpu....  13.4 us
    unnamed x1, local copies, waits for them, and re-layouts  0.68 us

profile of v5, /device:TPU:320, one launch (start us, length us, event | category | flops | bytes accessed | tf_op | source)
XLA Modules:
  0.0 14.1 jit_solution(17624637694378240303)
XLA Ops:
  0.0 13.4 %shard_map.55 = bf16[16,48,128]{2,1,0:T(8,128)(2,1)S(1)} custom-call(bf16[16,48,128]{2,1,0:T(8,128)(2,1)} %q_hbm.1, f32[1,16,48]{2,1,0:T(8,128)} %s_hbm.1, bf16[3,4,256,256]{3,2,1,0:T(8,128)(2,1)} %constant.6.clone.mx_hbm, bf16[8,4,64,144]{3,2,1,0:T(8,128)(2,1)} %constant.7.clone.ay_hbm, bf16[8,3,40,144]{3,2,1,0:T(8,128)(2,1)} %constant.8.clone.ac_hbm), custom_call_target="tpu_custom_call" | custom-call | tf_op jit(solution)/shard_map/pallas_call | solution.py:404
  13.4 0.7 %copy.7 = bf16[16,48,128]{2,1,0:T(8,128)(2,1)} copy(bf16[16,48,128]{2,1,0:T(8,128)(2,1)S(1)} %shard_map.55) | data formatting | bytes 393216

commit v6 on v5

--- a/solution.py
+++ b/solution.py
@@ -138,7 +138,8 @@
     qv, sv, mxv, ayv, acv, zh, zl, to_right, to_left, from_left, from_right,
     to_right_far, to_left_far, from_left_far, from_right_far, wide, wide2, yo,
     send0, send1, recv0, recv1, recv2, down2, up2, down3,
-    load_sem, xs_sem, xr_sem, ys_sem, yr_sem,
+    pass_down, pass_up, pass_down2,
+    load_sem, xs_sem, xr_sem, ys_sem, yr_sem, ps_sem, pr_sem,
 ):
     g, t = lax.axis_index("grp"), lax.axis_index("tile")
     right, left = lax.rem(t + 1, tiles), lax.rem(t + tiles - 1, tiles)
@@ -148,6 +149,9 @@
     has_left, has_right = t > 0, t < tiles - 1
     has_above, has_below = g > 0, g < groups - 1
     has_above2, has_below2 = g > 1, g < groups - 2
+    odd = lax.rem(t, 2) == 1
+    even = jnp.logical_not(odd)
+    also = lambda *conditions: functools.reduce(jnp.logical_and, conditions)
     barrier = pltpu.get_barrier_semaphore()
     for there, dev in (
         (has_left, (g, left)), (has_right, (g, right)),
@@ -174,6 +178,7 @@
         (has_above, (recv0.at[0], recv1.at[0], down2)),
         (has_below, (recv0.at[1], recv1.at[1], up2)),
         (has_above2, (recv2, down3)),
+        (jnp.logical_or(odd, has_left), (down2.at[0], up2.at[0], down3.at[0])),
     ):
         @pl.when(jnp.logical_not(there))
         def _():
@@ -239,11 +244,9 @@
         for to, _, c in copies:
             pl.when(to)(c.start)
 
-    def finish(copies):
-        for to, came, c in copies:
+    def arrived(copies):
+        for _, came, c in copies:
             pl.when(came)(c.wait_recv)
-        for to, came, c in copies:
-            pl.when(to)(c.wait_send)
 
     neighbours = (
         jnp.where(has_left, 1, 0) + jnp.where(has_right, 1, 0) + jnp.where(has_above, 1, 0)
@@ -251,9 +254,27 @@
     )
     pl.semaphore_wait(barrier, neighbours)
     farcopies = [
-        (has_right, has_left, remote(to_right_far, from_left_far, xs_sem.at[0], xr_sem.at[0], (g, right))),
-        (has_left, has_right, remote(to_left_far, from_right_far, xs_sem.at[1], xr_sem.at[1], (g, left))),
+        (also(even, has_right), also(odd, has_left), remote(to_right_far, from_left_far, xs_sem.at[0], xr_sem.at[0], (g, right))),
+        (also(even, has_left), also(odd, has_right), remote(to_left_far, from_right_far, xs_sem.at[1], xr_sem.at[1], (g, left))),
     ]
+
+    def along_y(k, far, down, up, down_2, send, recv, first):
+        return [
+            (also(odd, has_below), also(odd, has_above), remote(far.at[:16], down.at[k], send.at[first + k], recv.at[first + k], (below, t))),
+            (also(odd, has_above), also(odd, has_below), remote(far.at[8:], up.at[k], send.at[first + 2 + k], recv.at[first + 2 + k], (above, t))),
+            (also(odd, has_below2), also(odd, has_above2), remote(far.at[:8], down_2.at[k], send.at[first + 4 + k], recv.at[first + 4 + k], (below2, t))),
+        ]
+
+    own_far = [along_y(k, far, pass_down, pass_up, pass_down2, ps_sem, pr_sem, 0) for k, far in enumerate((to_right_far, to_left_far))]
+    relays = [along_y(k, far, down2, up2, down3, ys_sem, yr_sem, 5) for k, far in enumerate((from_left_far, from_right_far))]
+    forwards = []
+    for k, to, came, dev in ((0, has_right, has_left, (g, right)), (1, has_left, has_right, (g, left))):
+        forwards.append([
+            (also(odd, to, there), also(even, came, there), remote(src.at[k], dst.at[k], ps_sem.at[6 + 2 * i + k], yr_sem.at[5 + 2 * i + k], dev))
+            for i, (there, src, dst) in enumerate(((has_above, pass_down, down2), (has_below, pass_up, up2), (has_above2, pass_down2, down3)))
+        ])
+    start(own_far[0])
+    start(own_far[1])
     start(farcopies)
     xcopies = [
         (has_right, has_left, remote(to_right, from_left, xs_sem.at[2], xr_sem.at[2], (g, right))),
@@ -285,15 +306,14 @@
     ]
     start(y1copies)
 
-    finish(farcopies)
-    y2copies = []
-    for k, far in enumerate((from_left_far, from_right_far)):
-        y2copies += [
-            (has_below, has_above, remote(far.at[:16], down2.at[k], ys_sem.at[5 + k], yr_sem.at[5 + k], (below, t))),
-            (has_above, has_below, remote(far.at[8:], up2.at[k], ys_sem.at[7 + k], yr_sem.at[7 + k], (above, t))),
-            (has_below2, has_above2, remote(far.at[:8], down3.at[k], ys_sem.at[9 + k], yr_sem.at[9 + k], (below2, t))),
-        ]
-    start(y2copies)
+    arrived(farcopies[:1])
+    start(relays[0])
+    arrived(own_far[0])
+    start(forwards[0])
+    arrived(own_far[1])
+    start(forwards[1])
+    arrived(farcopies[1:])
+    start(relays[1])
 
     def spread(l, p, packed0, packed_r, packed_l, keep=None):
         win = 8 << l
@@ -305,7 +325,7 @@
         a = jnp.where(both(w < win), turned(packed_r, win * p + SR[l]), 0.0)
         return a + jnp.where(both(w >= BX - win), turned(packed_l, win * p + SL[l]), 0.0)
 
-    finish(xcopies)
+    arrived(xcopies)
     a, b = from_left[:24], from_right[:24]
     w = lanes_of((24, BX)) % 8 < 4
     wide[0, 0, :24] = jnp.where(w, a, b)
@@ -331,7 +351,7 @@
         yo[z] = value
 
     wide2[...] = jnp.zeros(wide2.shape, F32)
-    finish(y1copies)
+    arrived(y1copies)
     lane = lanes_of((1, BX))
 
     def valid(l, p, j, v):
@@ -366,7 +386,9 @@
         for r, vs in adds.items():
             yo[z, r : r + 1, :] = functools.reduce(lambda a, b: a + b, vs, yo[z, r : r + 1, :])
 
-    finish(y2copies)
+    for k in range(2):
+        arrived(relays[k])
+        arrived(forwards[k])
     for k in range(2):
         for l in range(1, LEVELS):
             n, rows = min(7, BY >> l), wide2.at[l - 1, k]
@@ -396,6 +418,9 @@
                 tiles[i] = tiles[i] + spread(l, p, None, a, b, keep)
         out_ref[z] = jnp.concatenate(tiles, axis=0).astype(BF16)
 
+    for to, _, c in sum(own_far + relays + forwards, farcopies + xcopies + y1copies):
+        pl.when(to)(c.wait_send)
+
 
 def body(quantized, scales):
     groups, tiles = lax.axis_size("grp"), lax.axis_size("tile")
@@ -427,7 +452,10 @@
             pltpu.VMEM((2, 16, BX), F32),
             pltpu.VMEM((2, 16, BX), F32),
             pltpu.VMEM((2, 8, BX), F32),
-            dma((5,)), dma((4,)), dma((4,)), dma((11,)), dma((11,)),
+            pltpu.VMEM((2, 16, BX), F32),
+            pltpu.VMEM((2, 16, BX), F32),
+            pltpu.VMEM((2, 8, BX), F32),
+            dma((5,)), dma((4,)), dma((4,)), dma((11,)), dma((11,)), dma((12,)), dma((6,)),
         ],
         compiler_params=pltpu.CompilerParams(collective_id=0, has_side_effects=True),
     )(quantized, scales, jnp.asarray(x_matrices()), jnp.asarray(y_matrices(groups)),

time: 14.2 us -> 13.8 us (0.972)
  the two profiles are of different devices: /device:TPU:320 before, /device:TPU:191 now
where the time goes in v6:
time: 13.8 us; the launch traced here: 13.7 us
  Pallas kernels  13 us (94%)
  local copies, waits for them, and re-layouts  0.68 us (5%)
    pallas_call x1, Pallas kernels, body(): pl.pallas_call(functools.partial(kernel, groups, tiles), out_shape=pltpu....  13 us
    unnamed x1, local copies, waits for them, and re-layouts  0.68 us

profile of v6, /device:TPU:191, one launch (start us, length us, event | category | flops | bytes accessed | tf_op | source)
XLA Modules:
  0.0 13.7 jit_solution(11775068148462688191)
XLA Ops:
  0.0 13.0 %shard_map.55 = bf16[16,48,128]{2,1,0:T(8,128)(2,1)S(1)} custom-call(bf16[16,48,128]{2,1,0:T(8,128)(2,1)} %q_hbm.1, f32[1,16,48]{2,1,0:T(8,128)} %s_hbm.1, bf16[3,4,256,256]{3,2,1,0:T(8,128)(2,1)} %constant.6.clone.mx_hbm, bf16[8,4,64,144]{3,2,1,0:T(8,128)(2,1)} %constant.7.clone.ay_hbm, bf16[8,3,40,144]{3,2,1,0:T(8,128)(2,1)} %constant.8.clone.ac_hbm), custom_call_target="tpu_custom_call" | custom-call | tf_op jit(solution)/shard_map/pallas_call | solution.py:429
  13.0 0.7 %copy.7 = bf16[16,48,128]{2,1,0:T(8,128)(2,1)} copy(bf16[16,48,128]{2,1,0:T(8,128)(2,1)S(1)} %shard_map.55) | data formatting | bytes 393216

commit v7 on v6

--- a/solution.py
+++ b/solution.py
@@ -132,12 +132,23 @@
     return lax.broadcasted_iota(jnp.int32, shape, len(shape) - 1)
 
 
+def spread(l, p, packed0, packed_r, packed_l, keep=None):
+    win = 8 << l
+    turned = lambda e, s: pltpu.roll(e, (-s) % BX, 1)
+    both = (lambda m: m) if keep is None else (lambda m: jnp.logical_and(m, keep))
+    if l == 0:
+        return jnp.where(both((lanes_of(packed0.shape) + 4) % BX < 8), turned(packed0, 8 * p), 0.0)
+    w = lanes_of(packed_r.shape)
+    a = jnp.where(both(w < win), turned(packed_r, win * p + SR[l]), 0.0)
+    return a + jnp.where(both(w >= BX - win), turned(packed_l, win * p + SL[l]), 0.0)
+
+
 def kernel(
     groups, tiles,
-    q_hbm, s_hbm, mx_hbm, ay_hbm, ac_hbm, out_ref,
+    q_hbm, s_hbm, mx_hbm, ay_hbm, ac_hbm, yo, down2, up2, down3,
     qv, sv, mxv, ayv, acv, zh, zl, to_right, to_left, from_left, from_right,
-    to_right_far, to_left_far, from_left_far, from_right_far, wide, wide2, yo,
-    send0, send1, recv0, recv1, recv2, down2, up2, down3,
+    to_right_far, to_left_far, from_left_far, from_right_far, wide, own_y,
+    send0, send1, recv0, recv1, recv2,
     pass_down, pass_up, pass_down2,
     load_sem, xs_sem, xr_sem, ys_sem, yr_sem, ps_sem, pr_sem,
 ):
@@ -287,7 +298,7 @@
         r = dot(ayv[l], stacked(jnp.concatenate([own[l][p] for p in range(n)], axis=1)))
         tail = [r[BY:, p * BX : (p + 1) * BX] for p in range(n)]
         for p in range(n):
-            yo[OFF[l] + p] = r[:BY, p * BX : (p + 1) * BX]
+            own_y[OFF[l] + p] = r[:BY, p * BX : (p + 1) * BX]
             if l == 0:
                 send0[0, p] = tail[p][:4]
                 send0[1, p] = tail[p][12:]
@@ -315,16 +326,6 @@
     arrived(farcopies[1:])
     start(relays[1])
 
-    def spread(l, p, packed0, packed_r, packed_l, keep=None):
-        win = 8 << l
-        turned = lambda e, s: pltpu.roll(e, (-s) % BX, 1)
-        both = (lambda m: m) if keep is None else (lambda m: jnp.logical_and(m, keep))
-        if l == 0:
-            return jnp.where(both((lanes_of(packed0.shape) + 4) % BX < 8), turned(packed0, 8 * p), 0.0)
-        w = lanes_of(packed_r.shape)
-        a = jnp.where(both(w < win), turned(packed_r, win * p + SR[l]), 0.0)
-        return a + jnp.where(both(w >= BX - win), turned(packed_l, win * p + SL[l]), 0.0)
-
     arrived(xcopies)
     a, b = from_left[:24], from_right[:24]
     w = lanes_of((24, BX)) % 8 < 4
@@ -342,7 +343,7 @@
             if z % (1 << l):
                 continue
             p = z >> l
-            part = yo[OFF[l] + p] + spread(l, p, wide[l, 0], wide[l, 0], wide[l, 1])
+            part = own_y[OFF[l] + p] + spread(l, p, wide[l, 0], wide[l, 0], wide[l, 1])
             if value is None:
                 value = part
             else:
@@ -350,7 +351,6 @@
                 value = jnp.where((row % step == 0) & (lane % step == 0), value, part)
         yo[z] = value
 
-    wide2[...] = jnp.zeros(wide2.shape, F32)
     arrived(y1copies)
     lane = lanes_of((1, BX))
 
@@ -386,9 +386,15 @@
         for r, vs in adds.items():
             yo[z, r : r + 1, :] = functools.reduce(lambda a, b: a + b, vs, yo[z, r : r + 1, :])
 
+    for to, _, c in sum(own_far + relays + forwards, farcopies + xcopies + y1copies):
+        pl.when(to)(c.wait_send)
     for k in range(2):
         arrived(relays[k])
         arrived(forwards[k])
+
+
+def last_kernel(yo, down2, up2, down3, out_hbm, wide2, rounded, sem):
+    wide2[...] = jnp.zeros(wide2.shape, F32)
     for k in range(2):
         for l in range(1, LEVELS):
             n, rows = min(7, BY >> l), wide2.at[l - 1, k]
@@ -401,7 +407,7 @@
     low = jnp.where(w % 8 < 4, up2[0, :8], up2[1, :8])
     ends = jnp.where(r < 4, top, low)
     not_lower = jnp.logical_or(r % 2 == 1, w % 2 == 1)
-    for z in range(NZ):
+    for z in (*range(1, NZ, 2), *range(0, NZ, 2)):
         tiles = [yo[z, 8 * i : 8 * i + 8, :] for i in range(6)]
         e = spread(0, z, ends, None, None, not_lower if z % 2 == 0 else None)
         tiles[0] = tiles[0] + jnp.where(r < 4, e, 0.0)
@@ -416,19 +422,23 @@
                     keep = jnp.logical_and(keep, jnp.logical_or(r % (2 << l) > 0, w % (2 << l) > 0))
                 a, b = (wide2[l - 1, k, 8 * i : 8 * i + 8, :] for k in range(2))
                 tiles[i] = tiles[i] + spread(l, p, None, a, b, keep)
-        out_ref[z] = jnp.concatenate(tiles, axis=0).astype(BF16)
-
-    for to, _, c in sum(own_far + relays + forwards, farcopies + xcopies + y1copies):
-        pl.when(to)(c.wait_send)
+        rounded[z] = jnp.concatenate(tiles, axis=0).astype(BF16)
+        pltpu.make_async_copy(rounded.at[z], out_hbm.at[z], sem.at[0]).start()
+    pltpu.make_async_copy(rounded, out_hbm, sem.at[0]).wait()
 
 
 def body(quantized, scales):
     groups, tiles = lax.axis_size("grp"), lax.axis_size("tile")
     hbm = pl.BlockSpec(memory_space=pl.ANY)
     dma = pltpu.SemaphoreType.DMA
-    return pl.pallas_call(
+    held = pl.pallas_call(
         functools.partial(kernel, groups, tiles),
-        out_shape=pltpu.VMEM((NZ, BY, BX), BF16),
+        out_shape=[
+            pltpu.VMEM((NZ, BY, BX), F32),
+            pltpu.VMEM((2, 16, BX), F32),
+            pltpu.VMEM((2, 16, BX), F32),
+            pltpu.VMEM((2, 8, BX), F32),
+        ],
         in_specs=[hbm] * 5,
 
         scratch_shapes=[
@@ -442,7 +452,6 @@
             *[pltpu.VMEM((BY, BX), F32) for _ in range(4)],
             *[pltpu.VMEM((24, BX), F32) for _ in range(4)],
             pltpu.VMEM((LEVELS, 2, BY, BX), F32),
-            pltpu.VMEM((LEVELS - 1, 2, BY, BX), F32),
             pltpu.VMEM((NP, BY, BX), F32),
             pltpu.VMEM((2, NZ, 4, BX), F32),
             pltpu.VMEM((2, 6, 8, BX), F32),
@@ -452,14 +461,23 @@
             pltpu.VMEM((2, 16, BX), F32),
             pltpu.VMEM((2, 16, BX), F32),
             pltpu.VMEM((2, 8, BX), F32),
-            pltpu.VMEM((2, 16, BX), F32),
-            pltpu.VMEM((2, 16, BX), F32),
-            pltpu.VMEM((2, 8, BX), F32),
             dma((5,)), dma((4,)), dma((4,)), dma((11,)), dma((11,)), dma((12,)), dma((6,)),
         ],
         compiler_params=pltpu.CompilerParams(collective_id=0, has_side_effects=True),
     )(quantized, scales, jnp.asarray(x_matrices()), jnp.asarray(y_matrices(groups)),
       jnp.asarray(packed_matrices(groups)))
+    return pl.pallas_call(
+        last_kernel,
+        out_shape=jax.ShapeDtypeStruct((NZ, BY, BX), BF16),
+        in_specs=[pl.BlockSpec(memory_space=pltpu.VMEM)] * 4,
+        out_specs=hbm,
+        scratch_shapes=[
+            pltpu.VMEM((LEVELS - 1, 2, BY, BX), F32),
+            pltpu.VMEM((NZ, BY, BX), BF16),
+            dma((1,)),
+        ],
+        compiler_params=pltpu.CompilerParams(vmem_limit_bytes=8 << 20),
+    )(*held)
 
 
 def solution(mesh):

time: 13.8 us -> 13.7 us (level)
  local copies, waits for them, and re-layouts: 0.68 us -> 0 us
  Pallas kernels: 13 us -> 13.6 us
    unnamed x1 -> x0, local copies, waits for them, and re-layouts: 0.68 us -> none
    pallas_call x1 -> x2, Pallas kernels: 13 us -> 13.6 us  [the longest x1 12.7 us: body(): pl.pallas_call(functools.partial(kernel, groups, tiles), out_shape=[pltpu...]
where the time goes in v7:
time: 13.7 us; the launch traced here: 13.6 us
  Pallas kernels  13.6 us (99%)
    pallas_call x1, Pallas kernels, body(): pl.pallas_call(functools.partial(kernel, groups, tiles), out_shape=[pltpu...  12.7 us
    pallas_call x1, Pallas kernels, body(): pl.pallas_call(last_kernel, out_shape=jax.ShapeDtypeStruct((NZ, BY, BX),...  0.84 us

profile of v7, /device:TPU:191, one launch (start us, length us, event | category | flops | bytes accessed | tf_op | source)
XLA Modules:
  0.0 13.6 jit_solution(3331229596945828098)
XLA Ops:
  0.0 12.7 %shard_map.55 = (f32[16,48,128]{2,1,0:T(8,128)S(1)}, f32[2,16,128]{2,1,0:T(8,128)S(1)}, f32[2,16,128]{2,1,0:T(8,128)S(1)}, f32[2,8,128]{2,1,0:T(8,128)S(1)}) custom-call(bf16[16,48,128]{2,1,0:T(8,128)(2,1)} %q_hbm.1, f32[1,16,48]{2,1,0:T(8,128)} %s_hbm.1, bf16[3,4,256,256]{3,2,1,0:T(8,128)(2,1)} %constant.6.clone.mx_hbm, ...), custom_call_target="tpu_custom_call" | custom-call | tf_op jit(solution)/shard_map/pallas_call | solution.py:434
  12.7 0.8 %shard_map.56 = bf16[16,48,128]{2,1,0:T(8,128)(2,1)} custom-call(f32[16,48,128]{2,1,0:T(8,128)S(1)} %get-tuple-element.9.yo, f32[2,16,128]{2,1,0:T(8,128)S(1)} %get-tuple-element.10.down2, f32[2,16,128]{2,1,0:T(8,128)S(1)} %get-tuple-element.11.up2, f32[2,8,128]{2,1,0:T(8,128)S(1)} %get-tuple-element.12.down3), custom_call_target="tpu_custom_call" | custom-call | tf_op jit(solution)/shard_map/pallas_call | solution.py:469

commit v8 on v7

--- a/solution.py
+++ b/solution.py
@@ -147,10 +147,10 @@
     groups, tiles,
     q_hbm, s_hbm, mx_hbm, ay_hbm, ac_hbm, yo, down2, up2, down3,
     qv, sv, mxv, ayv, acv, zh, zl, to_right, to_left, from_left, from_right,
-    to_right_far, to_left_far, from_left_far, from_right_far, wide, own_y,
+    to_right_far, to_left_far, wide, own_y,
     send0, send1, recv0, recv1, recv2,
-    pass_down, pass_up, pass_down2,
-    load_sem, xs_sem, xr_sem, ys_sem, yr_sem, ps_sem, pr_sem,
+    pass_down, pass_up, pass_down2, far3,
+    load_sem, xs_sem, xr_sem, ys_sem, yr_sem, ps_sem, pr_sem, ready,
 ):
     g, t = lax.axis_index("grp"), lax.axis_index("tile")
     right, left = lax.rem(t + 1, tiles), lax.rem(t + tiles - 1, tiles)
@@ -163,33 +163,42 @@
     odd = lax.rem(t, 2) == 1
     even = jnp.logical_not(odd)
     also = lambda *conditions: functools.reduce(jnp.logical_and, conditions)
+    half = groups // 2
+    jump = jnp.logical_and(g >= half - 2, g < half)
+    landed = jnp.logical_and(g >= half, g < half + 2)
     barrier = pltpu.get_barrier_semaphore()
     for there, dev in (
-        (has_left, (g, left)), (has_right, (g, right)),
+        (has_left, (g, left)), (also(odd, has_right), (g, right)),
         (has_above, (above, t)), (has_below, (below, t)),
         (has_above2, (above2, t)), (has_below2, (below2, t)),
+        *(
+            (also(odd, to, there), (y, x))
+            for to, x in ((has_left, left), (has_right, right))
+            for there, y in ((has_above, above), (has_below, below), (landed, above2))
+        ),
     ):
         @pl.when(there)
         def _():
             pl.semaphore_signal(barrier, inc=1, device_id=dev, device_id_type=MESH)
 
     side = jnp.where(t == 0, 0, jnp.where(t == tiles - 1, 2, 1))
+    matrices = [
+        pltpu.make_async_copy(mx_hbm.at[side, l], mxv.at[l], load_sem.at[4 + l]) for l in range(LEVELS)
+    ]
     loads = [
         pltpu.make_async_copy(q_hbm, qv, load_sem.at[0]),
         pltpu.make_async_copy(s_hbm, sv, load_sem.at[1]),
-        pltpu.make_async_copy(mx_hbm.at[side], mxv, load_sem.at[2]),
-        pltpu.make_async_copy(ay_hbm.at[g], ayv, load_sem.at[3]),
-        pltpu.make_async_copy(ac_hbm.at[g], acv, load_sem.at[4]),
+        pltpu.make_async_copy(ay_hbm.at[g], ayv, load_sem.at[2]),
+        pltpu.make_async_copy(ac_hbm.at[g], acv, load_sem.at[3]),
     ]
-    for c in loads:
+    for c in loads[:2] + matrices + loads[2:]:
         c.start()
     for there, buffers in (
-        (has_left, (from_left, from_left_far)),
-        (has_right, (from_right, from_right_far)),
+        (has_left, (from_left, down2.at[0], up2.at[0], down3.at[0])),
+        (has_right, (from_right, down2.at[1], up2.at[1], down3.at[1])),
         (has_above, (recv0.at[0], recv1.at[0], down2)),
         (has_below, (recv0.at[1], recv1.at[1], up2)),
         (has_above2, (recv2, down3)),
-        (jnp.logical_or(odd, has_left), (down2.at[0], up2.at[0], down3.at[0])),
     ):
         @pl.when(jnp.logical_not(there))
         def _():
@@ -210,7 +219,8 @@
                 zl[OFF[l] + p, rows, :] = lo
             band = band[0::2]
 
-    loads[2].wait()
+    for c in matrices + loads[2:]:
+        c.wait()
     own, packs = [], []
     lane = lanes_of((1, 1, BX))
     for l in range(LEVELS):
@@ -228,8 +238,6 @@
         which = lax.broadcasted_iota(jnp.int32, (n, 1, BX), 0)
         packs.append(jnp.sum(jnp.where(which == plane, r[:, BX:].reshape(n, BY, BX), 0.0), axis=0))
 
-    loads[3].wait()
-    loads[4].wait()
     e0 = dot(ayv[0], stacked(packs[0]))
     e1, e2, e3 = (dot(acv[l - 1], stacked(packs[l])) for l in range(1, LEVELS))
     lane = lanes_of((40, BX))
@@ -259,15 +267,28 @@
         for _, came, c in copies:
             pl.when(came)(c.wait_recv)
 
-    neighbours = (
-        jnp.where(has_left, 1, 0) + jnp.where(has_right, 1, 0) + jnp.where(has_above, 1, 0)
-        + jnp.where(has_below, 1, 0) + jnp.where(has_above2, 1, 0) + jnp.where(has_below2, 1, 0)
-    )
-    pl.semaphore_wait(barrier, neighbours)
-    farcopies = [
-        (also(even, has_right), also(odd, has_left), remote(to_right_far, from_left_far, xs_sem.at[0], xr_sem.at[0], (g, right))),
-        (also(even, has_left), also(odd, has_right), remote(to_left_far, from_right_far, xs_sem.at[1], xr_sem.at[1], (g, left))),
-    ]
+    one = lambda condition: jnp.where(condition, 1, 0)
+    sides = one(has_left) + one(has_right)
+    along = one(has_above) + one(has_below) + one(has_above2) + one(has_below2)
+    across = sides * (1 + one(has_above) + one(has_below) + one(jump))
+    pl.semaphore_wait(barrier, along + jnp.where(even, across, one(has_right)))
+
+    @pl.when(even)
+    def _():
+        pl.semaphore_signal(ready, inc=1, device_id=(g, right), device_id_type=MESH)
+
+    straight, second, relays = [], [], []
+    near2 = also(has_below2, jnp.logical_not(jump))
+    for k, far, to, came, x in (
+        (0, to_right_far, has_right, has_left, right), (1, to_left_far, has_left, has_right, left)
+    ):
+        straight += [
+            (also(even, to, has_below), also(odd, came, has_above), remote(far.at[:16], down2.at[k], ys_sem.at[5 + k], yr_sem.at[5 + k], (below, x))),
+            (also(even, to, has_above), also(odd, came, has_below), remote(far.at[8:], up2.at[k], ys_sem.at[7 + k], yr_sem.at[7 + k], (above, x))),
+            (also(even, to, jump), also(odd, came, landed), remote(far.at[:8], down3.at[k], ys_sem.at[9 + k], yr_sem.at[9 + k], (below2, x))),
+        ]
+        second.append((also(even, to, near2), also(odd, came, near2), remote(far.at[:8], far3.at[k], xs_sem.at[2 + k], xr_sem.at[2 + k], (g, x))))
+        relays.append((also(odd, came, near2), also(odd, came, has_above2, jnp.logical_not(landed)), remote(far3.at[k], down3.at[k], ys_sem.at[9 + k], yr_sem.at[9 + k], (below2, t))))
 
     def along_y(k, far, down, up, down_2, send, recv, first):
         return [
@@ -277,7 +298,6 @@
         ]
 
     own_far = [along_y(k, far, pass_down, pass_up, pass_down2, ps_sem, pr_sem, 0) for k, far in enumerate((to_right_far, to_left_far))]
-    relays = [along_y(k, far, down2, up2, down3, ys_sem, yr_sem, 5) for k, far in enumerate((from_left_far, from_right_far))]
     forwards = []
     for k, to, came, dev in ((0, has_right, has_left, (g, right)), (1, has_left, has_right, (g, left))):
         forwards.append([
@@ -286,12 +306,13 @@
         ])
     start(own_far[0])
     start(own_far[1])
-    start(farcopies)
+    start(straight)
+    start(second)
     xcopies = [
-        (has_right, has_left, remote(to_right, from_left, xs_sem.at[2], xr_sem.at[2], (g, right))),
-        (has_left, has_right, remote(to_left, from_right, xs_sem.at[3], xr_sem.at[3], (g, left))),
+        (has_right, has_left, remote(to_right, from_left, xs_sem.at[0], xr_sem.at[0], (g, right))),
+        (has_left, has_right, remote(to_left, from_right, xs_sem.at[1], xr_sem.at[1], (g, left))),
     ]
-    start(xcopies)
+    start([xcopies[0], (also(even, has_left), has_right, xcopies[1][2])])
 
     for l in range(LEVELS):
         n = NZ >> l
@@ -317,14 +338,20 @@
     ]
     start(y1copies)
 
-    arrived(farcopies[:1])
-    start(relays[0])
     arrived(own_far[0])
     start(forwards[0])
+    arrived(second[1:])
+    start(relays[1:])
+
+    @pl.when(odd)
+    def _():
+        pl.semaphore_wait(ready, 1)
+        xcopies[1][2].start()
+
     arrived(own_far[1])
     start(forwards[1])
-    arrived(farcopies[1:])
-    start(relays[1])
+    arrived(second[:1])
+    start(relays[:1])
 
     arrived(xcopies)
     a, b = from_left[:24], from_right[:24]
@@ -386,10 +413,11 @@
         for r, vs in adds.items():
             yo[z, r : r + 1, :] = functools.reduce(lambda a, b: a + b, vs, yo[z, r : r + 1, :])
 
-    for to, _, c in sum(own_far + relays + forwards, farcopies + xcopies + y1copies):
+    for to, _, c in sum(own_far + forwards, straight + second + relays + xcopies + y1copies):
         pl.when(to)(c.wait_send)
+    arrived(straight)
+    arrived(relays)
     for k in range(2):
-        arrived(relays[k])
         arrived(forwards[k])
 
 
@@ -450,7 +478,7 @@
             pltpu.VMEM((NP, BY, BX), BF16),
             pltpu.VMEM((NP, BY, BX), BF16),
             *[pltpu.VMEM((BY, BX), F32) for _ in range(4)],
-            *[pltpu.VMEM((24, BX), F32) for _ in range(4)],
+            *[pltpu.VMEM((24, BX), F32) for _ in range(2)],
             pltpu.VMEM((LEVELS, 2, BY, BX), F32),
             pltpu.VMEM((NP, BY, BX), F32),
             pltpu.VMEM((2, NZ, 4, BX), F32),
@@ -461,7 +489,9 @@
             pltpu.VMEM((2, 16, BX), F32),
             pltpu.VMEM((2, 16, BX), F32),
             pltpu.VMEM((2, 8, BX), F32),
-            dma((5,)), dma((4,)), dma((4,)), dma((11,)), dma((11,)), dma((12,)), dma((6,)),
+            pltpu.VMEM((2, 8, BX), F32),
+            dma((8,)), dma((4,)), dma((4,)), dma((11,)), dma((11,)), dma((12,)), dma((6,)),
+            pltpu.SemaphoreType.REGULAR,
         ],
         compiler_params=pltpu.CompilerParams(collective_id=0, has_side_effects=True),
     )(quantized, scales, jnp.asarray(x_matrices()), jnp.asarray(y_matrices(groups)),

time: 13.7 us -> 13.5 us (0.985)
  the two profiles are of different devices: /device:TPU:191 before, /device:TPU:320 now
where the time goes in v8:
time: 13.5 us; the launch traced here: 13.4 us
  Pallas kernels  13.4 us (99%)
    pallas_call x1, Pallas kernels, body(): pl.pallas_call(functools.partial(kernel, groups, tiles), out_shape=[pltpu...  12.6 us
    pallas_call x1, Pallas kernels, body(): pl.pallas_call(last_kernel, out_shape=jax.ShapeDtypeStruct((NZ, BY, BX),...  0.84 us

profile of v8, /device:TPU:320, one launch (start us, length us, event | category | flops | bytes accessed | tf_op | source)
XLA Modules:
  0.0 13.4 jit_solution(4234213824398170511)
XLA Ops:
  0.0 12.6 %shard_map.55 = (f32[16,48,128]{2,1,0:T(8,128)S(1)}, f32[2,16,128]{2,1,0:T(8,128)S(1)}, f32[2,16,128]{2,1,0:T(8,128)S(1)}, f32[2,8,128]{2,1,0:T(8,128)S(1)}) custom-call(bf16[16,48,128]{2,1,0:T(8,128)(2,1)} %q_hbm.1, f32[1,16,48]{2,1,0:T(8,128)} %s_hbm.1, bf16[3,4,256,256]{3,2,1,0:T(8,128)(2,1)} %constant.6.clone.mx_hbm, ...), custom_call_target="tpu_custom_call" | custom-call | tf_op jit(solution)/shard_map/pallas_call | solution.py:462
  12.6 0.8 %shard_map.56 = bf16[16,48,128]{2,1,0:T(8,128)(2,1)} custom-call(f32[16,48,128]{2,1,0:T(8,128)S(1)} %get-tuple-element.9.yo, f32[2,16,128]{2,1,0:T(8,128)S(1)} %get-tuple-element.10.down2, f32[2,16,128]{2,1,0:T(8,128)S(1)} %get-tuple-element.11.up2, f32[2,8,128]{2,1,0:T(8,128)S(1)} %get-tuple-element.12.down3), custom_call_target="tpu_custom_call" | custom-call | tf_op jit(solution)/shard_map/pallas_call | solution.py:499

commit v9 on v8

--- a/solution.py
+++ b/solution.py
@@ -338,8 +338,9 @@
     ]
     start(y1copies)
 
-    arrived(own_far[0])
-    start(forwards[0])
+    for came, on in zip(own_far[0], forwards[0]):
+        arrived([came])
+        start([on])
     arrived(second[1:])
     start(relays[1:])
 
@@ -348,8 +349,9 @@
         pl.semaphore_wait(ready, 1)
         xcopies[1][2].start()
 
-    arrived(own_far[1])
-    start(forwards[1])
+    for came, on in zip(own_far[1], forwards[1]):
+        arrived([came])
+        start([on])
     arrived(second[:1])
     start(relays[:1])
 

time: 13.5 us -> 13.5 us (level)
  no operation moved by 1% of the time
where the time goes in v9:
time: 13.5 us; the launch traced here: 13.4 us
  Pallas kernels  13.4 us (99%)
    pallas_call x1, Pallas kernels, body(): pl.pallas_call(functools.partial(kernel, groups, tiles), out_shape=[pltpu...  12.6 us
    pallas_call x1, Pallas kernels, body(): pl.pallas_call(last_kernel, out_shape=jax.ShapeDtypeStruct((NZ, BY, BX),...  0.84 us

profile of v9, /device:TPU:320, one launch (start us, length us, event | category | flops | bytes accessed | tf_op | source)
XLA Modules:
  0.0 13.4 jit_solution(5060720459940195519)
XLA Ops:
  0.0 12.6 %shard_map.55 = (f32[16,48,128]{2,1,0:T(8,128)S(1)}, f32[2,16,128]{2,1,0:T(8,128)S(1)}, f32[2,16,128]{2,1,0:T(8,128)S(1)}, f32[2,8,128]{2,1,0:T(8,128)S(1)}) custom-call(bf16[16,48,128]{2,1,0:T(8,128)(2,1)} %q_hbm.1, f32[1,16,48]{2,1,0:T(8,128)} %s_hbm.1, bf16[3,4,256,256]{3,2,1,0:T(8,128)(2,1)} %constant.6.clone.mx_hbm, ...), custom_call_target="tpu_custom_call" | custom-call | tf_op jit(solution)/shard_map/pallas_call | solution.py:464
  12.6 0.8 %shard_map.56 = bf16[16,48,128]{2,1,0:T(8,128)(2,1)} custom-call(f32[16,48,128]{2,1,0:T(8,128)S(1)} %get-tuple-element.9.yo, f32[2,16,128]{2,1,0:T(8,128)S(1)} %get-tuple-element.10.down2, f32[2,16,128]{2,1,0:T(8,128)S(1)} %get-tuple-element.11.up2, f32[2,8,128]{2,1,0:T(8,128)S(1)} %get-tuple-element.12.down3), custom_call_target="tpu_custom_call" | custom-call | tf_op jit(solution)/shard_map/pallas_call | solution.py:501
